TPU v7x, 32 devices: a whole 2x2x4 slice. The times are simulated.
32 devices in a mesh: range: 8 (over z, y), depth: 4 (over x, core).
Axes of the slice: x: 2, y: 2, z: 4, core: 2. Of those that a mesh axis runs over, the one named last changes fastest.
Arguments:
- pressure: float32 [4096, 1024], P('depth', 'range'), may hold values from -6 to 6
- vel_range: float32 [4096, 1024], P('depth', 'range'), may hold values from -3 to 3
- vel_depth: float32 [4096, 1024], P('depth', 'range'), may hold values from -3 to 3
- sound_speed: float32 [4096, 1024], P('depth', 'range'), may hold values from 0.5 to 1.1
- density: float32 [4096, 1024], P('depth', 'range'), may hold values from 1 to 3
- ahead_speed: float32 [4096, 64], P('depth'), may hold values from 0.5 to 1.1
- ahead_density: float32 [4096, 64], P('depth'), may hold values from 1 to 3
- shifts: int32 [4], replicated, may hold values from 1 to 16, as said below
- sources: int32 [8, 2], replicated, may hold values from 0 to 4095, as said below
- wavelet: float32 [8, 4], replicated, may hold values from -12 to 12
Outputs:
- pressure_out: float32 [4096, 1024], P('depth', 'range')
- range_out: float32 [4096, 1024], P('depth', 'range')
- depth_out: float32 [4096, 1024], P('depth', 'range')
Inputs may be any that keep to these rules, and one draw needn't show every extreme that they name: `shifts`: every draw has a step that advances by exactly 16 columns. `sources`: column 0 is a depth index below 4096, column 1 a range index below 1024.
All inputs are finite; a program needn't handle non-finite values.
Results may differ from a plain program's by a relative error of at most 0.0003.
Values sent between devices are 32-bit elements; how exact they have to be, the bound alone decides.
No kernel may reach another device: no remote copies, remote signals or barrier semaphores. Data moves between devices by JAX's collectives and lax.ppermute only.
A program may use at most 64 MiB of HBM per device.

v0:
```python
import functools

import jax
import jax.numpy as jnp
from jax import lax
from jax.experimental import pallas as pl
from jax.experimental.pallas import tpu as pltpu
from jax.sharding import PartitionSpec as P

ITERS = 4
TIME_STEP = 0.6
LANES = 128
TILE = 8
MARGIN = 16
SKEW = 4
WIDTH = 42
STRIP = 16
BLOCKS = LANES // STRIP
KEPT = LANES - STRIP // 2
BLOCK = 1024


def lane_ids(rows):
    return lax.broadcasted_iota(jnp.int32, (rows, LANES), 1)


def between(lanes, low, high):
    return jnp.logical_and(lanes >= low, lanes < high)


def roll(x, by):
    return pltpu.roll(x, by % LANES, 1)


def for_rows(start, stop, fn, size=BLOCK):
    whole = (stop - start) // size

    def step(i, carry):
        fn(pl.multiple_of(start + i * size, TILE), size)
        return carry

    if whole > 1:
        lax.fori_loop(0, whole, step, 0)
    elif whole == 1:
        fn(start, size)
    if start + whole * size < stop:
        fn(start + whole * size, stop - start - whole * size)


def offsets_of(shifts):
    found = [jnp.int32(0)]
    for t in range(ITERS):
        found.append(found[-1] + shifts[t])
    return found


def range_ends():
    place = lax.axis_index("range")
    return place == 0, place == lax.axis_size("range") - 1


def depth_ends():
    place = lax.axis_index("depth")
    return place == 0, place == lax.axis_size("depth") - 1


def set_coefs(start, stop, c, rho, ax, az, stiff):
    def coefs(r, k):
        here = pl.ds(r, k)
        dense = rho[here, :]
        ax[here, :] = (2.0 * TIME_STEP) / (dense + roll(dense, -1))
        az[here, :] = (2.0 * TIME_STEP) / (dense + rho[pl.ds(r + 1, k), :])
        if c is not None:
            speed = c[here, :]
            stiff[here, :] = TIME_STEP * (dense * speed * speed)

    for_rows(start, stop, coefs)


def find_sources(sources, first_row, places):
    found = []
    for k in range(sources.shape[1]):
        for row, lane, good in places(sources[0, k] - first_row, sources[1, k]):
            good = jnp.logical_and(good, jnp.logical_and(lane >= 0, lane < LANES))
            found.append((k, row, lane, good))
    return found


def inject(field, found, wavelet, t, reach=None):
    here_any = functools.reduce(jnp.logical_or, [good for _, _, _, good in found])

    @pl.when(here_any)
    def _():
        rows = lax.broadcasted_iota(jnp.int32, (TILE, LANES), 0)
        lanes = lane_ids(TILE)
        for k, row, lane, good in found:
            if reach is not None:
                good = jnp.logical_and(good, lane % STRIP <= reach)

            @pl.when(good)
            def _(k=k, row=row, lane=lane):
                at = pl.ds(pl.multiple_of((row // TILE) * TILE, TILE), TILE)
                here = jnp.logical_and(rows == row % TILE, lanes == lane)
                field[at, :] = field[at, :] + jnp.where(here, wavelet[t, k], 0.0)


def left_steps(n, fields, coefs, stages, shifts, found, wavelet):
    ax, az, stiff = coefs
    ps, us, ws = stages
    offsets = offsets_of(shifts)
    at_start, _ = range_ends()
    for t in range(ITERS):
        p, u, w = fields if t == 0 else (ps.at[t - 1], us.at[t - 1], ws.at[t - 1])
        u_new, w_new, p_new = us.at[t], ws.at[t], ps.at[t]
        wall = jnp.where(at_start, offsets[t], -1)

        def speeds(r, k):
            here = pl.ds(r, k)
            now = p[here, :]
            u_new[here, :] = u[here, :] - ax[here, :] * (roll(now, -1) - now)
            w_new[here, :] = w[here, :] - az[here, :] * (p[pl.ds(r + 1, k), :] - now)

        def press(r, k):
            here = pl.ds(r, k)
            fast = u_new[here, :]
            left = jnp.where(lane_ids(k) == wall, 0.0, roll(fast, 1))
            down = w_new[here, :] - w_new[pl.ds(r - 1, k), :]
            p_new[here, :] = p[here, :] - stiff[here, :] * ((fast - left) + down)

        for_rows(0, n - TILE, speeds)
        for_rows(TILE, n - TILE, press)
        inject(p_new, found, wavelet, t)


def slanted(here, p0, stages, stiff):
    ps, us, ws = stages
    lanes = lane_ids(TILE)

    def pick(parts):
        found = parts[-1]
        for t in range(len(parts) - 2, -1, -1):
            found = jnp.where(lanes <= t, parts[t], found)
        return found

    a = pick([p0[here, :]] + [ps[t, here, :] for t in range(ITERS - 1)])
    b = pick([us[t, here, :] for t in range(ITERS)])
    c = pick([ws[t, here, :] for t in range(ITERS)])
    found = jnp.where(lanes < 3 * SKEW, roll(c, 2 * SKEW), roll(stiff, 3 * SKEW))
    found = jnp.where(lanes < 2 * SKEW, roll(b, SKEW), found)
    return jnp.where(lanes < SKEW, a, found)


def packed(p, u, w):
    lanes = lane_ids(p.shape[0])
    found = jnp.where(
        between(lanes, SKEW, SKEW + 2 * WIDTH), roll(u, WIDTH), roll(w, 2 * WIDTH)
    )
    return jnp.where(between(lanes, SKEW, SKEW + WIDTH), p, found)


def finals(stages, here):
    return [stage[ITERS - 1, here, :] for stage in stages]


def own_kernel(height, *refs):
    arrays, ahead = refs[3:8], refs[8:10]
    plane, to_up, to_down = refs[10:13]
    own, stages, scalars, flag = refs[13:18], refs[18:21], refs[21:24], refs[24]
    ax, az, stiff, ends, sems, end_sems, scalar_sems = refs[25:]
    shifts, sources, wavelet = scalars
    order = (4, 3, 0, 1, 2)
    copies = {k: pltpu.make_async_copy(arrays[k], own[k], sems.at[k]) for k in order}
    for k in order:
        copies[k].start()
    scalar_copies = [
        pltpu.make_async_copy(refs[k], scalars[k], scalar_sems.at[k]) for k in range(3)
    ]
    for copy in scalar_copies:
        copy.start()
    end_copies = []
    for side, start in enumerate((0, height - LANES)):
        for f in range(2):
            copy = pltpu.make_async_copy(
                ahead[f].at[:, pl.ds(start, LANES)],
                ends.at[side, pl.ds(f * LANES // 2, LANES // 2), :],
                end_sems.at[side, f],
            )
            copy.start()
            end_copies.append(copy)
    p, u, w, c, rho = own

    def place(row, col):
        return [(row, col - lax.axis_index("range") * LANES, between(row, 0, height))]

    copies[4].wait()
    copies[3].wait()
    set_coefs(0, height - TILE, c, rho, ax, az, stiff)
    for copy in scalar_copies:
        copy.wait()
    flag[0] = jnp.where(offsets_of(shifts)[ITERS] > SKEW + WIDTH, 1, 0)
    found = find_sources(sources, lax.axis_index("depth") * height, place)
    for k in (0, 1, 2):
        copies[k].wait()
    left_steps(height, (p, u, w), (ax, az, stiff), stages, shifts, found, wavelet)

    def finish(r, k):
        plane[pl.ds(r - MARGIN, k), :] = packed(*finals(stages, pl.ds(r, k)))

    for_rows(MARGIN, height - MARGIN, finish)
    for copy in end_copies:
        copy.wait()
    for k in range(5):
        to_up[pl.ds(k * TILE, TILE), :] = own[k][pl.ds(0, TILE), :]
        to_down[pl.ds(k * TILE, TILE), :] = own[k][pl.ds(height - TILE, TILE), :]
    at = pl.ds(5 * TILE, TILE)
    to_up[at, :] = ends[0].T[:TILE]
    to_down[at, :] = ends[1].T[LANES - TILE :]


def own_stiff(own, here):
    speed = own[3][here, :]
    return TIME_STEP * (own[4][here, :] * speed * speed)


def lean_kernel(height, *refs):
    own, stages, lean = refs[:5], refs[5:8], refs[8]
    each = height // BLOCKS
    tiles = each // TILE + 2

    def tile(i, slot):
        lanes = lane_ids(TILE)
        found = rhos = None
        for b in range(BLOCKS):
            row = b * each + i * TILE - TILE
            if not isinstance(i, int):
                row = pl.multiple_of(row, TILE)
            elif row < 0 or row >= height:
                row = 0
            here = pl.ds(row, TILE)
            part = slanted(here, own[0], stages, own_stiff(own, here))
            part = roll(part, STRIP * b) if b else part
            dense = roll(own[4][here, :], 4 * BLOCKS * slot + SKEW * b)
            found = part if b == 0 else jnp.where(lanes < STRIP * b, found, part)
            rhos = dense if b == 0 else jnp.where(lanes < 4 * BLOCKS * slot + SKEW * b, rhos, dense)
        lean[pl.ds(i * TILE, TILE), :] = found
        return rhos

    def group_of(first, count, out):
        lanes = lane_ids(TILE)
        total = None
        for slot in range(count):
            rhos = tile(first + slot, slot)
            total = rhos if slot == 0 else jnp.where(lanes < 4 * BLOCKS * slot, total, rhos)
        lean[pl.ds((tiles + out) * TILE, TILE), :] = total

    groups = (tiles - 2) // 4

    def body(m, carry):
        group_of(1 + 4 * m, 4, m)
        return carry

    lax.fori_loop(0, groups, body, 0)
    lanes = lane_ids(TILE)
    total = jnp.where(lanes < 4 * BLOCKS, tile(0, 0), tile(tiles - 1, 1))
    lean[pl.ds((tiles + groups) * TILE, TILE), :] = total


def ghost_rows(up, down, k, last_own):
    at_top, at_bottom = depth_ends()
    at = pl.ds(k * TILE, TILE)
    above, below = up[at, :], down[at, :]
    if k == 4:
        above = jnp.where(at_top, 1.0, above)
        below = jnp.where(at_bottom, last_own, below)
    return above, below


def edge_kernel(height, *refs):
    shifts, sources, wavelet = refs[:3]
    own, up, down = refs[3:8], refs[8], refs[9]
    out, done = refs[10:12]
    ax, az, stiff = refs[12:15]
    stages, inner = refs[15:18], refs[18:23]
    seg = 3 * MARGIN
    n = 2 * seg
    low = height - 2 * MARGIN
    for k in range(5):
        filler = jnp.full((TILE, LANES), 1.0 if k == 4 else 0.0, jnp.float32)
        last_own = jnp.broadcast_to(own[k][pl.ds(height - 1, 1), :], (TILE, LANES))
        above, below = ghost_rows(up, down, k, last_own)
        inner[k][pl.ds(0, TILE), :] = filler
        inner[k][pl.ds(TILE, TILE), :] = above
        inner[k][pl.ds(2 * TILE, 2 * MARGIN), :] = own[k][pl.ds(0, 2 * MARGIN), :]
        inner[k][pl.ds(seg, 2 * MARGIN), :] = own[k][pl.ds(low, 2 * MARGIN), :]
        inner[k][pl.ds(n - 2 * TILE, TILE), :] = below
        inner[k][pl.ds(n - TILE, TILE), :] = filler
    p, u, w, c, rho = inner
    set_coefs(0, n - TILE, c, rho, ax, az, stiff)
    at_top, _ = depth_ends()
    at = pl.ds(TILE, TILE)
    az[at, :] = jnp.where(at_top, 0.0, az[at, :])

    def place(row, col):
        upper = between(row, -TILE, 2 * MARGIN)
        lower = between(row, low, height + TILE)
        local = jnp.where(upper, row + MARGIN, row - low + seg)
        lane = col - lax.axis_index("range") * LANES
        return [(local, lane, jnp.logical_or(upper, lower))]

    found = find_sources(sources, lax.axis_index("depth") * height, place)
    left_steps(n, (p, u, w), (ax, az, stiff), stages, shifts, found, wavelet)
    for side, start in enumerate((MARGIN, seg + MARGIN)):
        fields = finals(stages, pl.ds(start, MARGIN))
        there = pl.ds(side * MARGIN, MARGIN)
        out[there, :] = packed(*fields)
        for f in range(3):
            done[f, there, :] = fields[f]
    lanes = lane_ids(TILE)
    found = None
    for side, start in enumerate((TILE, seg + MARGIN)):
        for j in range(3):
            here = pl.ds(start + j * TILE, TILE)
            part = jnp.where(
                lanes < 4 * SKEW,
                slanted(here, p, stages, stiff[here, :]),
                roll(rho[here, :], 4 * SKEW),
            )
            lane = 5 * SKEW * (3 * side + j)
            part = roll(part, lane) if lane else part
            found = part if lane == 0 else jnp.where(lanes < lane, found, part)
    out[pl.ds(2 * MARGIN, TILE), :] = found


def rho_slot(i, tiles):
    if i == 0:
        return (tiles - 2) // 4, 0
    if i == tiles - 1:
        return (tiles - 2) // 4, 1
    return (i - 1) // 4, (i - 1) % 4


def wide_kernel(height, *refs):
    shifts, sources, wavelet = refs[:3]
    own, ahead, up, down = refs[3:8], refs[8:10], refs[10], refs[11]
    strip, out = refs[12:14]
    p, u, w = out.at[0], out.at[1], out.at[2]
    rho, ax, az, al, stiff, raw, sems = refs[14:]
    half = LANES // 2
    n = height + 2 * MARGIN
    at_top, at_bottom = depth_ends()
    _, at_end = range_ends()

    @pl.when(jnp.logical_not(at_end))
    def _():
        each = height // BLOCKS
        rows = each + 2 * TILE

        def put(i, k, parts):
            lanes = lane_ids(k)
            for a in range(5):
                found = None
                for b in range(BLOCKS):
                    part = roll(parts[b][a], STRIP * b - KEPT)
                    found = part if b == 0 else jnp.where(lanes < STRIP * b, found, part)
                strip[a, pl.ds(i + TILE, k), :] = found

        def fields(here):
            return [own[0][here, :], own[1][here, :], own[2][here, :], own_stiff(own, here), own[4][here, :]]

        def middle(i, k):
            put(i, k, [fields(pl.ds(b * each - TILE + i, k)) for b in range(BLOCKS)])

        for_rows(TILE, rows - TILE, middle, 32)
        above, below = [], []
        for k in range(5):
            last_own = jnp.broadcast_to(own[k][pl.ds(height - 1, 1), :], (TILE, LANES))
            one, two = ghost_rows(up, down, k, last_own)
            above.append(one)
            below.append(two)
        for parts in (above, below):
            parts[3] = TIME_STEP * (parts[4] * parts[3] * parts[3])
        inner = [fields(pl.ds(b * each - TILE, TILE)) for b in range(1, BLOCKS)]
        put(0, TILE, [above] + inner)
        inner = [fields(pl.ds((b + 1) * each, TILE)) for b in range(BLOCKS - 1)]
        put(rows - TILE, TILE, inner + [below])

    @pl.when(at_end)
    def _():
        copies = [pltpu.make_async_copy(ahead[f], raw.at[f], sems.at[f]) for f in range(2)]
        for copy in copies:
            copy.start()
        for copy in copies:
            copy.wait()

        def place_rows(e, k, parts, both):
            here = pl.ds(e, k)
            lanes = lane_ids(k)
            mine = lanes < half
            for ref, part in zip((p, u, w), parts):
                ref[here, :] = jnp.where(mine, roll(part, half), 0.0)
            dense = jnp.where(mine, roll(parts[4], half), both)
            speed = roll(jnp.where(mine, both, parts[3]), half)
            rho[here, :] = dense
            stiff[here, :] = TIME_STEP * (dense * speed * speed)

        for j in range(height // LANES):
            at = pl.ds(j * LANES, LANES)
            both = jnp.concatenate([raw[0, :, at], raw[1, :, at]], 0).T
            place_rows(j * LANES + MARGIN, LANES, [ref[at, :] for ref in own], both)
        above, below = [], []
        for k in range(5):
            last_own = jnp.broadcast_to(own[k][pl.ds(height - 1, 1), :], (TILE, LANES))
            one, two = ghost_rows(up, down, k, last_own)
            above.append(one)
            below.append(two)
        at = pl.ds(5 * TILE, TILE)
        lanes = lane_ids(TILE)
        one, two = up[at, :], down[at, :]
        last = jnp.broadcast_to(rho[pl.ds(height + MARGIN - 1, 1), :], (TILE, LANES))
        one = jnp.where(jnp.logical_and(at_top, lanes >= half), 1.0, one)
        two = jnp.where(jnp.logical_and(at_bottom, lanes >= half), last, two)
        place_rows(TILE, TILE, above, one)
        place_rows(height + MARGIN, TILE, below, two)
        for e in (0, n - TILE):
            here = pl.ds(e, TILE)
            for ref in (p, u, w, stiff):
                ref[here, :] = jnp.zeros((TILE, LANES), jnp.float32)
            rho[here, :] = jnp.ones((TILE, LANES), jnp.float32)
        set_coefs(0, n - TILE, None, rho, ax, az, None)

        def edge_coefs(r, k):
            al[pl.ds(r, k), :] = TIME_STEP / rho[pl.ds(r, k), :]

        for_rows(0, n - TILE, edge_coefs)
        at = pl.ds(TILE, TILE)
        az[at, :] = jnp.where(at_top, 0.0, az[at, :])

        def place(row, col):
            good = between(row, -TILE, height + TILE)
            return [(row + MARGIN, col - lax.axis_index("range") * LANES - half, good)]

        found = find_sources(sources, lax.axis_index("depth") * height, place)
        offsets = offsets_of(shifts)
        for t in range(ITERS):
            edge = half - 1 + offsets[t]

            def speeds(r, k):
                here = pl.ds(r, k)
                lanes = lane_ids(k)
                now = p[here, :]
                slope = jnp.where(lanes == edge, al[here, :], ax[here, :])
                slope = jnp.where(lanes > edge, 0.0, slope)
                u[here, :] = u[here, :] - slope * (roll(now, -1) - now)
                slope = jnp.where(lanes > edge, 0.0, az[here, :])
                w[here, :] = w[here, :] - slope * (p[pl.ds(r + 1, k), :] - now)

            def press(r, k):
                here = pl.ds(r, k)
                fast = u[here, :]
                down_ = w[here, :] - w[pl.ds(r - 1, k), :]
                hard = jnp.where(lane_ids(k) > edge, 0.0, stiff[here, :])
                p[here, :] = p[here, :] - hard * ((fast - roll(fast, 1)) + down_)

            for_rows(0, n - TILE, speeds)
            for_rows(TILE, n - TILE, press)
            inject(p, found, wavelet, t)


def rest_kernel(height, extra, *refs):
    stages, done, out = refs[:3], refs[3], refs[4]
    more = extra - SKEW - WIDTH
    start = SKEW + WIDTH
    half = height // 2

    def read(row, k):
        if isinstance(row, int) and row < MARGIN:
            return [done[f, pl.ds(row, k), :] for f in range(3)]
        if isinstance(row, int) and row >= height - MARGIN:
            return [done[f, pl.ds(row - height + 2 * MARGIN, k), :] for f in range(3)]
        return finals(stages, pl.ds(row, k))

    def join(fields):
        lanes = lane_ids(fields[0].shape[0])
        found = jnp.where(lanes < start + 2 * more, roll(fields[1], more), roll(fields[2], 2 * more))
        return jnp.where(lanes < start + more, fields[0], found)

    def beside(r, k):
        inner = between(lane_ids(k), start, start + 3 * more)
        out[pl.ds(r, k), :] = jnp.where(inner, join(read(r, k)), roll(join(read(r + half, k)), LANES // 2))

    beside(0, MARGIN)
    for_rows(MARGIN, half - MARGIN, beside, 96)
    beside(half - MARGIN, MARGIN)


def mid_kernel(height, *refs):
    shifts, stages, done, wide, near = refs[0], refs[1:4], refs[4], refs[5], refs[6]
    built = refs[7:]
    _, at_end = range_ends()
    total = offsets_of(shifts)[ITERS]
    turn = LANES - total
    inside = (MARGIN, height - MARGIN)

    @pl.when(jnp.logical_not(at_end))
    def _():
        def build(r, k):
            got = near[pl.ds(r - MARGIN, k), :]
            theirs = between(lane_ids(k), SKEW, total)
            for f in range(3):
                mine = stages[f][ITERS - 1, pl.ds(r, k), :]
                other = roll(got, -WIDTH * f) if f else got
                built[f][pl.ds(r, k), :] = pltpu.roll(jnp.where(theirs, other, mine), turn, 1)

        for_rows(*inside, build)

    @pl.when(at_end)
    def _():
        def build(r, k):
            lanes = lane_ids(k)
            inner = jnp.logical_and(lanes >= total, lanes < KEPT + SKEW)
            for f in range(3):
                part = roll(wide[f, pl.ds(r + MARGIN, k), :], LANES // 2)
                if inside[0] <= r < inside[1]:
                    mine = stages[f][ITERS - 1, pl.ds(r, k), :]
                else:
                    mine = done[f, pl.ds(0 if r < MARGIN else MARGIN, k), :]
                built[f][pl.ds(r, k), :] = pltpu.roll(jnp.where(inner, mine, part), turn, 1)

        build(0, MARGIN)
        build(MARGIN, height - 2 * MARGIN)
        build(height - MARGIN, MARGIN)


def last_kernel(height, extra, far_too, *refs):
    shifts, sources, wavelet = refs[:3]
    done, strip, lean, edge = refs[3:7]
    drafts = refs[7:10]
    rest = refs[10] if far_too else None
    refs = refs[10 + far_too :]
    outs, built = refs[:3], refs[3:6]
    p, u, w, rho, ax, az, stiff, gp, gu, gw, sems = refs[6:]
    at_top, _ = depth_ends()
    _, at_end = range_ends()
    each = height // BLOCKS
    tiles = each // TILE + 2
    n = (tiles + 2) * TILE
    half = LANES // 2
    own_part = STRIP // 2
    total = offsets_of(shifts)[ITERS]
    more = extra - SKEW - WIDTH
    start = SKEW + WIDTH
    turn = LANES - total

    @pl.when(at_end)
    def _():
        copies = [pltpu.make_async_copy(drafts[f], outs[f], sems.at[f, 0]) for f in range(3)]
        for copy in copies:
            copy.start()
        for copy in copies:
            copy.wait()

    @pl.when(jnp.logical_not(at_end))
    def _():
        lanes = lane_ids(TILE)
        inner = lanes % STRIP
        mine, ghost = inner < own_part, inner < own_part + SKEW
        fill = [0.0, 0.0, 0.0, 0.0, 1.0]
        six = edge[pl.ds(2 * MARGIN, TILE), :]
        for i in range(tiles):
            here = pl.ds((i + 1) * TILE, TILE)
            pack = lean[pl.ds(i * TILE, TILE), :]
            group, slot = rho_slot(i, tiles)
            dense = lean[pl.ds((tiles + group) * TILE, TILE), :]
            origin = 4 * BLOCKS * slot + SKEW * (lanes // STRIP) + inner - own_part
            theirs = jnp.take_along_axis(dense, jnp.clip(origin, 0, LANES - 1), 1)
            parts = [roll(pack, own_part - SKEW * g) if g != 2 else pack for g in range(4)]
            parts.append(theirs)
            late = None
            if i < 3:
                late, lane, b = 5 * SKEW * i, own_part, 0
            elif i >= tiles - 3:
                late, lane, b = 5 * SKEW * (i - tiles + 6), STRIP * (BLOCKS - 1) + own_part, BLOCKS - 1
            if late is not None:
                block = between(lanes, STRIP * b, STRIP * (b + 1))
                parts = [
                    jnp.where(block, roll(six, lane - late - SKEW * g), part)
                    for g, part in enumerate(parts)
                ]
            for ref, part in zip((gp, gu, gw), parts):
                ref[here, :] = part
            for a, (ref, part) in enumerate(zip((p, u, w, stiff, rho), parts)):
                other = jnp.where(ghost, part, fill[a])
                ref[here, :] = jnp.where(mine, strip[a, here, :], other)
        for e in (0, n - TILE):
            here = pl.ds(e, TILE)
            for ref in (p, u, w, stiff):
                ref[here, :] = jnp.zeros((TILE, LANES), jnp.float32)
            rho[here, :] = jnp.ones((TILE, LANES), jnp.float32)
        set_coefs(TILE, n - TILE, None, rho, ax, az, None)
        at = pl.ds(TILE, TILE)
        az[at, :] = jnp.where(jnp.logical_and(at_top, lane_ids(TILE) < STRIP), 0.0, az[at, :])

        def place(row, col):
            col = col - lax.axis_index("range") * LANES - KEPT
            inside = between(col, 0, STRIP)
            inside = jnp.logical_and(inside, between(row, -TILE, height + TILE))
            b = (row + TILE) // each
            local = row + TILE - b * each
            one = jnp.logical_and(inside, b < BLOCKS)
            two = jnp.logical_and(inside, jnp.logical_and(b > 0, local < 2 * TILE))
            return [
                (local + TILE, STRIP * b + col, one),
                (local + each + TILE, STRIP * (b - 1) + col, two),
            ]

        found = find_sources(sources, lax.axis_index("depth") * height, place)
        for t in range(ITERS):
            taken = own_part + t

            def speeds(r, k):
                here = pl.ds(r, k)
                inner = lane_ids(k) % STRIP
                now = p[here, :]
                fast = u[here, :] - ax[here, :] * (roll(now, -1) - now)
                u[here, :] = jnp.where(inner == taken, gu[here, :], fast)
                deep = w[here, :] - az[here, :] * (p[pl.ds(r + 1, k), :] - now)
                w[here, :] = jnp.where(inner == taken, gw[here, :], deep)

            def press(r, k):
                here = pl.ds(r, k)
                inner = lane_ids(k) % STRIP
                fast = u[here, :]
                down_ = w[here, :] - w[pl.ds(r - 1, k), :]
                new = p[here, :] - stiff[here, :] * ((fast - roll(fast, 1)) + down_)
                if t < ITERS - 1:
                    new = jnp.where(inner == taken + 1, gp[here, :], new)
                p[here, :] = new

            for_rows(TILE, n - TILE, speeds)
            for_rows(TILE, n - TILE, press)
            inject(p, found, wavelet, t, taken)

        copies = []
        for b in range(BLOCKS):
            first = b * each
            low, high = first, first + each
            edges = []
            if b == 0:
                low = MARGIN
                edges = [(0, 0)]
            if b == BLOCKS - 1:
                high = height - MARGIN
                edges = [(high, MARGIN)]

            def far_values(row, k):
                if row < height // 2:
                    return rest[pl.ds(row, k), :]
                return roll(rest[pl.ds(row - height // 2, k), :], half)

            for row, side in edges:
                here, there = pl.ds(row, MARGIN), pl.ds(side, MARGIN)
                lanes = lane_ids(MARGIN)
                for f, ref in enumerate((p, u, w)):
                    part = roll(ref[pl.ds(row - first + 2 * TILE, MARGIN), :], KEPT - STRIP * b)
                    kept = jnp.where(between(lanes, SKEW, KEPT + SKEW), done[f, there, :], part)
                    other = edge[there, :]
                    other = roll(other, -WIDTH * f) if f else other
                    if far_too:
                        far = far_values(row, MARGIN)
                        far = roll(far, -more * f) if f else far
                        other = jnp.where(lanes < start, other, far)
                    kept = jnp.where(between(lanes, SKEW, total), other, kept)
                    built[f][here, :] = pltpu.roll(kept, turn, 1)
            here, k = pl.ds(low, high - low), high - low
            natural = (lane_ids(k) + total) % LANES
            ready = between(natural, SKEW, KEPT + SKEW)
            shift = (KEPT - STRIP * b + LANES + turn) % LANES
            for f, ref in enumerate((p, u, w)):
                part = pltpu.roll(ref[pl.ds(low - first + 2 * TILE, k), :], shift, 1)
                kept = jnp.where(ready, drafts[f][here, :], part)
                if far_too:
                    far = pltpu.roll(far_values(low, k), (turn + LANES - more * f) % LANES, 1)
                    kept = jnp.where(between(natural, start, total), far, kept)
                built[f][here, :] = kept
            for f in range(3):
                at = pl.ds(first, each)
                copy = pltpu.make_async_copy(built[f].at[at, :], outs[f].at[at, :], sems.at[f, b])
                copy.start()
                copies.append(copy)
        for copy in copies:
            copy.wait()


def moved(x, axis, by):
    size = lax.axis_size(axis)
    pairs = [(i, i + by) for i in range(size) if 0 <= i + by < size]
    return lax.ppermute(x, axis, pairs)


LOCAL = pl.BlockSpec(memory_space=pltpu.VMEM)
REMOTE = pl.BlockSpec(memory_space=pl.ANY)
SCALAR = pl.BlockSpec(memory_space=pltpu.SMEM)


def shaped(shape, space):
    if space is SCALAR:
        return pltpu.SMEM(*shape)
    if space is LOCAL:
        return pltpu.VMEM(shape, jnp.float32)
    return jax.ShapeDtypeStruct(shape, jnp.float32)


def call(kernel, ins, outs, scratch=()):
    values, specs = [], []
    for value, space in ins:
        if space is LOCAL:
            value = pltpu.with_memory_space_constraint(value, pltpu.VMEM)
        elif space is SCALAR:
            value = pltpu.with_memory_space_constraint(value, pltpu.SMEM)
        elif space is REMOTE:
            value = pltpu.with_memory_space_constraint(value, pltpu.HBM)
        values.append(value)
        specs.append(space)
    return pl.pallas_call(
        kernel,
        in_specs=specs,
        out_specs=[space for _, space in outs],
        out_shape=[shaped(*pair) for pair in outs],
        scratch_shapes=list(scratch),
        compiler_params=pltpu.CompilerParams(vmem_limit_bytes=8 * 1024 * 1024),
    )(*values)


def room(*shape):
    return pltpu.VMEM(shape, jnp.float32)


def shards(
    pressure,
    vel_range,
    vel_depth,
    sound_speed,
    density,
    ahead_speed,
    ahead_density,
    shifts,
    sources,
    wavelet,
):
    height, breadth = pressure.shape
    extra = ahead_speed.shape[1]
    assert breadth == LANES and 2 * extra == LANES and height % 512 == 0
    arrays = [(x, REMOTE) for x in (pressure, vel_range, vel_depth, sound_speed, density)]
    ahead = [(x.T, REMOTE) for x in (ahead_speed, ahead_density)]
    small = [(shifts, REMOTE), (sources.T, REMOTE), (wavelet.T, REMOTE)]
    sizes = (shifts.shape, sources.shape[::-1], wavelet.shape[::-1])
    kinds = (jnp.int32, jnp.int32, jnp.float32)
    scalars = [(pair, SCALAR) for pair in zip(sizes, kinds)]
    field = (height, LANES)
    dma = pltpu.SemaphoreType.DMA

    found = call(
        functools.partial(own_kernel, height),
        small + arrays + ahead,
        [((height - 2 * MARGIN, LANES), LOCAL)]
        + [((6 * TILE, LANES), LOCAL)] * 2
        + [(field, LOCAL)] * 5
        + [((ITERS, *field), LOCAL)] * 3
        + scalars
        + [(((1,), jnp.int32), SCALAR)],
        [room(*field)] * 3 + [room(2, LANES, LANES), dma((5,)), dma((2, 2)), dma((3,))],
    )
    tiles = height // BLOCKS // TILE + 2
    lean_rows = (tiles + (tiles - 2) // 4 + 1) * TILE
    n_edge = 6 * MARGIN
    n_wide = height + 2 * MARGIN
    n_strip = (tiles + 2) * TILE

    def finish(more, ahead, plane, to_up, to_down, *found):
        ahead = [(x, REMOTE) for x in ahead]
        own = [(x, LOCAL) for x in found[:5]]
        stages = [(x, LOCAL) for x in found[5:8]]
        small = [(x, SCALAR) for x in found[8:]]
        near = moved(plane, "range", -1)
        down = moved(to_up, "depth", -1)
        up = moved(to_down, "depth", 1)
        (lean,) = call(
            functools.partial(lean_kernel, height), own + stages, [((lean_rows, LANES), LOCAL)]
        )
        lean_near = moved(lean, "range", -1)
        sides = [(up, LOCAL), (down, LOCAL)]
        edge, done = call(
            functools.partial(edge_kernel, height),
            small + own + sides,
            [((2 * MARGIN + TILE, LANES), LOCAL), ((3, 2 * MARGIN, LANES), LOCAL)],
            [room(n_edge, LANES)] * 3
            + [room(ITERS, n_edge, LANES)] * 3
            + [room(n_edge, LANES)] * 5,
        )
        edge_near = moved(edge, "range", -1)
        received = []
        if more:
            (rest,) = call(
                functools.partial(rest_kernel, height, extra),
                stages + [(done, LOCAL)],
                [((height // 2, LANES), LOCAL)],
            )
            received = [(moved(rest, "range", -1), LOCAL)]
        strip, wide = call(
            functools.partial(wide_kernel, height),
            small + own + ahead + sides,
            [((5, n_strip, LANES), LOCAL), ((3, n_wide, LANES), LOCAL)],
            [room(n_wide, LANES)] * 5 + [room(2, extra, height), dma((2,))],
        )
        drafts = call(
            functools.partial(mid_kernel, height),
            small[:1] + stages + [(x, LOCAL) for x in (done, wide, near)],
            [(field, LOCAL)] * 3,
        )
        mixed = [(x, LOCAL) for x in (done, strip, lean_near, edge_near, *drafts)]
        return tuple(
            call(
                functools.partial(last_kernel, height, extra, more),
                small + mixed + received,
                [(field, REMOTE)] * 3,
                [room(*field)] * 3 + [room(n_strip, LANES)] * 10 + [dma((3, BLOCKS))],
            )
        )

    return lax.cond(
        found[-1].reshape(()) > 0,
        functools.partial(finish, True),
        functools.partial(finish, False),
        [x for x, _ in ahead],
        *found[:-1],
    )


def solution(mesh):
    field = P("depth", "range")
    strip = P("depth", None)
    return jax.shard_map(
        shards,
        mesh=mesh,
        in_specs=(field,) * 5 + (strip,) * 2 + (P(),) * 3,
        out_specs=(field,) * 3,
        check_vma=False,
    )
```

profile of v0, /device:TPU:29, one launch (start us, length us, event | category | flops | bytes accessed | tf_op | source)
XLA Modules:
  0.0 31.6 jit_solution(15617206779635757688)
XLA Ops:
  0.6 3.9 %shard_map.127 = (f32[992,128]{1,0:T(8,128)S(1)}, f32[48,128]{1,0:T(8,128)S(1)}, f32[48,128]{1,0:T(8,128)S(1)}, f32[1024,128]{1,0:T(8,128)S(1)}, f32[1024,128]{1...) custom-call(s32[4]{0:T(128)} %refs_0_.1, ...), custom_call_target="tpu_custom_call" | custom-call | tf_op jit(solution)/shard_map/pallas_call | solution.py:724
  4.6 26.8 %conditional.1 = ((f32[1024,128]{1,0:T(8,128)}, f32[1024,128]{1,0:T(8,128)}, f32[1024,128]{1,0:T(8,128)})) conditional(s32[]{:T(128)} %bitcast.4, (f32[48,128]{1,0:T(8,128)S(1)}, f32[48,128]{1,0:T(8,128)S(1)}, s32[4]{0:T(128)S(4)}, s32[2,8]{1,0:T(2,128)S(4)}, f32[4,8]{1,0:T(4,128)S(4)}, /*index=5*/f32[1024,128]{1,0:T(8,128)S(1)}, ...), branch_computations={%region_0.0_spmd, %region_1.0_spmd} | conditional | bytes 3735800 | solution.py:830
  4.6 2.2 %collective-permute-start.4 = (f32[992,128]{1,0:T(8,128)S(1)}, f32[992,128]{1,0:T(8,128)S(1)}, u32[]{:S(2)}, u32[]{:S(2)}) collective-permute-start(f32[992,128]{1,0:T(8,128)S(1)} %get-tuple-element.83), channel_id=1, source_target_pairs={{4,0},{8,4},{12,8},{16,12},{20,16},{24,20},{28,24},{5,1},{9,5},{13... | collective-permute-start | bytes 1523720 | tf_op jit(solution)/shard_map/cond/branch_0_fun/ppermute | solution.py:697
  6.8 2.1 %branch_0_fun.7 = f32[184,128]{1,0:T(8,128)S(1)} custom-call(f32[1024,128]{1,0:T(8,128)S(1)} %get-tuple-element.67.refs_3_.refs_0_, f32[1024,128]{1,0:T(8,128)S(1)} %get-tuple-element.68.refs_4_.refs_1_, f32[1024,128]{1,0:T(8,128)S(1)} %get-tuple-element.69.refs_5_.refs_2_, f32[1024,128]{1,0:T(8,128)S(1)} %get-tuple-element.70.refs_6_.refs_3_, ...), custom_call_target="tpu_custom_call" | custom-call | tf_op jit(solution)/shard_map/cond/branch_0_fun/pallas_call | solution.py:724
  8.9 3.0 %collective-permute-start.2 = (f32[184,128]{1,0:T(8,128)S(1)}, f32[184,128]{1,0:T(8,128)S(1)}, u32[]{:S(2)}, u32[]{:S(2)}) collective-permute-start(f32[184,128]{1,0:T(8,128)S(1)} %branch_0_fun.7), channel_id=1, source_target_pairs={{4,0},{8,4},{12,8},{16,12},{20,16},{24,20},{28,24},{5,1},{9,5},{13... | collective-permute-start | bytes 282632 | tf_op jit(solution)/shard_map/cond/branch_0_fun/ppermute | solution.py:697
  11.9 4.2 %collective-permute-start = (f32[48,128]{1,0:T(8,128)S(1)}, f32[48,128]{1,0:T(8,128)S(1)}, u32[]{:S(2)}, u32[]{:S(2)}) collective-permute-start(f32[48,128]{1,0:T(8,128)S(1)} %get-tuple-element.72), channel_id=1, source_target_pairs={{0,1},{1,2},{2,3},{4,5},{5,6},{6,7},{8,9},{9,10},{10,11},{12,13},{... | collective-permute-start | bytes 73736 | tf_op jit(solution)/shard_map/cond/branch_0_fun/ppermute | solution.py:697
  16.1 1.9 %collective-permute-start.1 = (f32[48,128]{1,0:T(8,128)S(1)}, f32[48,128]{1,0:T(8,128)S(1)}, u32[]{:S(2)}, u32[]{:S(2)}) collective-permute-start(f32[48,128]{1,0:T(8,128)S(1)} %get-tuple-element.73), channel_id=1, source_target_pairs={{1,0},{2,1},{3,2},{5,4},{6,5},{7,6},{9,8},{10,9},{11,10},{13,12},{... | collective-permute-start | bytes 73736 | tf_op jit(solution)/shard_map/cond/branch_0_fun/ppermute | solution.py:697
  18.1 0.0 collective-permute-done.refs_8_.refs_10_
  18.1 3.2 %collective-permute-done.1.refs_9_.refs_11_ = f32[48,128]{1,0:T(8,128)S(1)} collective-permute-done((f32[48,128]{1,0:T(8,128)S(1)}, f32[48,128]{1,0:T(8,128)S(1)}, u32[]{:S(2)}, u32[]{:S(2)}) %collective-permute-start.1) | collective-permute-done | bytes 24608 | tf_op jit(solution)/shard_map/cond/branch_0_fun/ppermute | solution.py:697
  21.3 0.8 %branch_0_fun.5 = (f32[40,128]{1,0:T(8,128)S(1)}, f32[3,32,128]{2,1,0:T(8,128)S(1)}) custom-call(s32[4]{0:T(128)S(4)} %get-tuple-element.64.refs_0_, s32[2,8]{1,0:T(2,128)S(4)} %get-tuple-element.65.refs_1_, f32[4,8]{1,0:T(4,128)S(4)} %get-tuple-element.66.refs_2_, f32[1024,128]{1,0:T(8,128)S(1)} %get-tuple-element.67.refs_3_.refs_0_, ...), custom_call_target="tpu_custom_call" | custom-call | tf_op jit(solution)/shard_map/cond/branch_0_fun/pallas_call | solution.py:724
  22.1 2.6 %collective-permute-start.3 = (f32[40,128]{1,0:T(8,128)S(1)}, f32[40,128]{1,0:T(8,128)S(1)}, u32[]{:S(2)}, u32[]{:S(2)}) collective-permute-start(f32[40,128]{1,0:T(8,128)S(1)} %get-tuple-element.81), channel_id=1, source_target_pairs={{4,0},{8,4},{12,8},{16,12},{20,16},{24,20},{28,24},{5,1},{9,5},{13... | collective-permute-start | bytes 61448 | tf_op jit(solution)/shard_map/cond/branch_0_fun/ppermute | solution.py:697
  24.7 4.1 %branch_0_fun.6 = (f32[5,160,128]{2,1,0:T(8,128)S(1)}, f32[3,1056,128]{2,1,0:T(8,128)S(1)}) custom-call(s32[4]{0:T(128)S(4)} %get-tuple-element.64.refs_0_, s32[2,8]{1,0:T(2,128)S(4)} %get-tuple-element.65.refs_1_, f32[4,8]{1,0:T(4,128)S(4)} %get-tuple-element.66.refs_2_, f32[1024,128]{1,0:T(8,128)S(1)} %get-tuple-element.67.refs_3_.refs_0_, ...), custom_call_target="tpu_custom_call" | custom-call | tf_op jit(solution)/shard_map/cond/branch_0_fun/pallas_call | solution.py:724
  28.8 0.0 collective-permute-done.4.refs_6_
  28.9 0.9 %branch_0_fun.8 = (f32[1024,128]{1,0:T(8,128)S(1)}, f32[1024,128]{1,0:T(8,128)S(1)}, f32[1024,128]{1,0:T(8,128)S(1)}) custom-call(s32[4]{0:T(128)S(4)} %get-tuple-element.64.refs_0_, f32[4,1024,128]{2,1,0:T(8,128)S(1)} %get-tuple-element.78.refs_5_.refs_1_, f32[4,1024,128]{2,1,0:T(8,128)S(1)} %get-tuple-element.79.refs_6_.refs_2_, ...), custom_call_target="tpu_custom_call" | custom-call | tf_op jit(solution)/shard_map/cond/branch_0_fun/pallas_call | solution.py:724
  29.8 0.0 collective-permute-done.3.refs_6_
  29.8 0.0 collective-permute-done.2.refs_5_
  29.8 1.4 %branch_0_fun.9 = (f32[1024,128]{1,0:T(8,128)}, f32[1024,128]{1,0:T(8,128)}, f32[1024,128]{1,0:T(8,128)}) custom-call(s32[4]{0:T(128)S(4)} %get-tuple-element.64.refs_0_, s32[2,8]{1,0:T(2,128)S(4)} %get-tuple-element.65.refs_1_, f32[4,8]{1,0:T(4,128)S(4)} %get-tuple-element.66.refs_2_, f32[3,32,128]{2,1,0:T(8,128)S(1)} %get-tuple-element.74.refs_4_.refs_3_, ...), custom_call_target="tpu_custom_call" | custom-call | tf_op jit(solution)/shard_map/cond/branch_0_fun/pallas_call | solution.py:724
Async XLA Ops:
  4.6 24.3 %collective-permute-start.4 = (f32[992,128]{1,0:T(8,128)S(1)}, f32[992,128]{1,0:T(8,128)S(1)}, u32[]{:S(2)}, u32[]{:S(2)}) collective-permute-start(f32[992,128]{1,0:T(8,128)S(1)} %get-tuple-element.83), channel_id=1, source_target_pairs={{4,0},{8,4},{12,8},{16,12},{20,16},{24,20},{28,24},{5,1},{9,5},{13... | collective-permute-start | bytes 1523720 | tf_op jit(solution)/shard_map/cond/branch_0_fun/ppermute | solution.py:697
  8.9 20.9 %collective-permute-start.2 = (f32[184,128]{1,0:T(8,128)S(1)}, f32[184,128]{1,0:T(8,128)S(1)}, u32[]{:S(2)}, u32[]{:S(2)}) collective-permute-start(f32[184,128]{1,0:T(8,128)S(1)} %branch_0_fun.7), channel_id=1, source_target_pairs={{4,0},{8,4},{12,8},{16,12},{20,16},{24,20},{28,24},{5,1},{9,5},{13... | collective-permute-start | bytes 282632 | tf_op jit(solution)/shard_map/cond/branch_0_fun/ppermute | solution.py:697
  11.9 6.2 %collective-permute-start = (f32[48,128]{1,0:T(8,128)S(1)}, f32[48,128]{1,0:T(8,128)S(1)}, u32[]{:S(2)}, u32[]{:S(2)}) collective-permute-start(f32[48,128]{1,0:T(8,128)S(1)} %get-tuple-element.72), channel_id=1, source_target_pairs={{0,1},{1,2},{2,3},{4,5},{5,6},{6,7},{8,9},{9,10},{10,11},{12,13},{... | collective-permute-start | bytes 73736 | tf_op jit(solution)/shard_map/cond/branch_0_fun/ppermute | solution.py:697
  16.1 5.1 %collective-permute-start.1 = (f32[48,128]{1,0:T(8,128)S(1)}, f32[48,128]{1,0:T(8,128)S(1)}, u32[]{:S(2)}, u32[]{:S(2)}) collective-permute-start(f32[48,128]{1,0:T(8,128)S(1)} %get-tuple-element.73), channel_id=1, source_target_pairs={{1,0},{2,1},{3,2},{5,4},{6,5},{7,6},{9,8},{10,9},{11,10},{13,12},{... | collective-permute-start | bytes 73736 | tf_op jit(solution)/shard_map/cond/branch_0_fun/ppermute | solution.py:697
  22.1 7.7 %collective-permute-start.3 = (f32[40,128]{1,0:T(8,128)S(1)}, f32[40,128]{1,0:T(8,128)S(1)}, u32[]{:S(2)}, u32[]{:S(2)}) collective-permute-start(f32[40,128]{1,0:T(8,128)S(1)} %get-tuple-element.81), channel_id=1, source_target_pairs={{4,0},{8,4},{12,8},{16,12},{20,16},{24,20},{28,24},{5,1},{9,5},{13... | collective-permute-start | bytes 61448 | tf_op jit(solution)/shard_map/cond/branch_0_fun/ppermute | solution.py:697
where the time goes:
time: 31.8 us; the launch traced here: 31.6 us
  starting transfers between devices  13.9 us (44%)
  Pallas kernels  13.3 us (42%)
  waiting for transfers between devices  3.22 us (10%)
  between operations  0.83 us (3%)
  loops' own time  0.32 us (1%)
    ppermute x5, starting transfers between devices, moved(): return lax.ppermute(x, axis, pairs)  13.9 us
    pallas_call x6, Pallas kernels, call(): pl.pallas_call(kernel, in_specs=specs, out_specs=[space for _, space in o...  13.3 us
    ppermute x5, waiting for transfers between devices, moved(): return lax.ppermute(x, axis, pairs)  3.22 us
  transfers between devices with their start and end apart: 5, of which 1 were waited for; matrix products, arithmetic and copies ran while one was open for 0% of the time, Pallas kernels for 25%

commit v1 on v0

--- a/solution.py
+++ b/solution.py
@@ -164,7 +164,7 @@
 
 def own_kernel(height, *refs):
     arrays, ahead = refs[3:8], refs[8:10]
-    plane, to_up, to_down = refs[10:13]
+    plane, swap_one, swap_two = refs[10:13]
     own, stages, scalars, flag = refs[13:18], refs[18:21], refs[21:24], refs[24]
     ax, az, stiff, ends, sems, end_sems, scalar_sems = refs[25:]
     shifts, sources, wavelet = scalars
@@ -209,12 +209,13 @@
     for_rows(MARGIN, height - MARGIN, finish)
     for copy in end_copies:
         copy.wait()
-    for k in range(5):
-        to_up[pl.ds(k * TILE, TILE), :] = own[k][pl.ds(0, TILE), :]
-        to_down[pl.ds(k * TILE, TILE), :] = own[k][pl.ds(height - TILE, TILE), :]
-    at = pl.ds(5 * TILE, TILE)
-    to_up[at, :] = ends[0].T[:TILE]
-    to_down[at, :] = ends[1].T[LANES - TILE :]
+    even = lax.axis_index("depth") % 2 == 0
+    tops = [own[k][pl.ds(0, TILE), :] for k in range(5)] + [ends[0].T[:TILE]]
+    lows = [own[k][pl.ds(height - TILE, TILE), :] for k in range(5)] + [ends[1].T[LANES - TILE :]]
+    for k, (top, low) in enumerate(zip(tops, lows)):
+        at = pl.ds(k * TILE, TILE)
+        swap_one[at, :] = jnp.where(even, low, top)
+        swap_two[at, :] = jnp.where(even, top, low)
 
 
 def own_stiff(own, here):
@@ -265,10 +266,16 @@
     lean[pl.ds((tiles + groups) * TILE, TILE), :] = total
 
 
-def ghost_rows(up, down, k, last_own):
+def swapped_rows(one, two, k):
+    at = pl.ds(k * TILE, TILE)
+    even = lax.axis_index("depth") % 2 == 0
+    first, second = one[at, :], two[at, :]
+    return jnp.where(even, second, first), jnp.where(even, first, second)
+
+
+def ghost_rows(one, two, k, last_own):
     at_top, at_bottom = depth_ends()
-    at = pl.ds(k * TILE, TILE)
-    above, below = up[at, :], down[at, :]
+    above, below = swapped_rows(one, two, k)
     if k == 4:
         above = jnp.where(at_top, 1.0, above)
         below = jnp.where(at_bottom, last_own, below)
@@ -277,17 +284,17 @@
 
 def edge_kernel(height, *refs):
     shifts, sources, wavelet = refs[:3]
-    own, up, down = refs[3:8], refs[8], refs[9]
-    out, done = refs[10:12]
-    ax, az, stiff = refs[12:15]
-    stages, inner = refs[15:18], refs[18:23]
+    own, swap_one, swap_two, lean = refs[3:8], refs[8], refs[9], refs[10]
+    out, done = refs[11:13]
+    ax, az, stiff = refs[13:16]
+    stages, inner = refs[16:19], refs[19:24]
     seg = 3 * MARGIN
     n = 2 * seg
     low = height - 2 * MARGIN
     for k in range(5):
         filler = jnp.full((TILE, LANES), 1.0 if k == 4 else 0.0, jnp.float32)
         last_own = jnp.broadcast_to(own[k][pl.ds(height - 1, 1), :], (TILE, LANES))
-        above, below = ghost_rows(up, down, k, last_own)
+        above, below = ghost_rows(swap_one, swap_two, k, last_own)
         inner[k][pl.ds(0, TILE), :] = filler
         inner[k][pl.ds(TILE, TILE), :] = above
         inner[k][pl.ds(2 * TILE, 2 * MARGIN), :] = own[k][pl.ds(0, 2 * MARGIN), :]
@@ -329,6 +336,7 @@
             part = roll(part, lane) if lane else part
             found = part if lane == 0 else jnp.where(lanes < lane, found, part)
     out[pl.ds(2 * MARGIN, TILE), :] = found
+    out[pl.ds(2 * MARGIN + TILE, lean.shape[0]), :] = lean[...]
 
 
 def rho_slot(i, tiles):
@@ -341,7 +349,7 @@
 
 def wide_kernel(height, *refs):
     shifts, sources, wavelet = refs[:3]
-    own, ahead, up, down = refs[3:8], refs[8:10], refs[10], refs[11]
+    own, ahead, swap_one, swap_two = refs[3:8], refs[8:10], refs[10], refs[11]
     strip, out = refs[12:14]
     p, u, w = out.at[0], out.at[1], out.at[2]
     rho, ax, az, al, stiff, raw, sems = refs[14:]
@@ -374,7 +382,7 @@
         above, below = [], []
         for k in range(5):
             last_own = jnp.broadcast_to(own[k][pl.ds(height - 1, 1), :], (TILE, LANES))
-            one, two = ghost_rows(up, down, k, last_own)
+            one, two = ghost_rows(swap_one, swap_two, k, last_own)
             above.append(one)
             below.append(two)
         for parts in (above, below):
@@ -410,12 +418,11 @@
         above, below = [], []
         for k in range(5):
             last_own = jnp.broadcast_to(own[k][pl.ds(height - 1, 1), :], (TILE, LANES))
-            one, two = ghost_rows(up, down, k, last_own)
+            one, two = ghost_rows(swap_one, swap_two, k, last_own)
             above.append(one)
             below.append(two)
-        at = pl.ds(5 * TILE, TILE)
         lanes = lane_ids(TILE)
-        one, two = up[at, :], down[at, :]
+        one, two = swapped_rows(swap_one, swap_two, 5)
         last = jnp.broadcast_to(rho[pl.ds(height + MARGIN - 1, 1), :], (TILE, LANES))
         one = jnp.where(jnp.logical_and(at_top, lanes >= half), 1.0, one)
         two = jnp.where(jnp.logical_and(at_bottom, lanes >= half), last, two)
@@ -533,10 +540,11 @@
 
 def last_kernel(height, extra, far_too, *refs):
     shifts, sources, wavelet = refs[:3]
-    done, strip, lean, edge = refs[3:7]
-    drafts = refs[7:10]
-    rest = refs[10] if far_too else None
-    refs = refs[10 + far_too :]
+    done, strip, edge = refs[3:6]
+    lean = edge.at[pl.ds(2 * MARGIN + TILE, edge.shape[0] - 2 * MARGIN - TILE)]
+    drafts = refs[6:9]
+    rest = refs[9] if far_too else None
+    refs = refs[9 + far_too :]
     outs, built = refs[:3], refs[3:6]
     p, u, w, rho, ax, az, stiff, gp, gu, gw, sems = refs[6:]
     at_top, _ = depth_ends()
@@ -691,10 +699,13 @@
             copy.wait()
 
 
-def moved(x, axis, by):
-    size = lax.axis_size(axis)
-    pairs = [(i, i + by) for i in range(size) if 0 <= i + by < size]
-    return lax.ppermute(x, axis, pairs)
+def moved(x):
+    return lax.ppermute(x, "range", [(i + 1, i) for i in range(lax.axis_size("range") - 1)])
+
+
+def swapped(x, first):
+    pairs = [(i, i + 1) for i in range(first, lax.axis_size("depth") - 1, 2)]
+    return lax.ppermute(x, "depth", pairs + [(j, i) for i, j in pairs])
 
 
 LOCAL = pl.BlockSpec(memory_space=pltpu.VMEM)
@@ -776,28 +787,25 @@
     n_wide = height + 2 * MARGIN
     n_strip = (tiles + 2) * TILE
 
-    def finish(more, ahead, plane, to_up, to_down, *found):
+    def finish(more, ahead, plane, swap_one, swap_two, *found):
         ahead = [(x, REMOTE) for x in ahead]
         own = [(x, LOCAL) for x in found[:5]]
         stages = [(x, LOCAL) for x in found[5:8]]
         small = [(x, SCALAR) for x in found[8:]]
-        near = moved(plane, "range", -1)
-        down = moved(to_up, "depth", -1)
-        up = moved(to_down, "depth", 1)
+        near = moved(plane)
+        sides = [(swapped(swap_one, 0), LOCAL), (swapped(swap_two, 1), LOCAL)]
         (lean,) = call(
             functools.partial(lean_kernel, height), own + stages, [((lean_rows, LANES), LOCAL)]
         )
-        lean_near = moved(lean, "range", -1)
-        sides = [(up, LOCAL), (down, LOCAL)]
         edge, done = call(
             functools.partial(edge_kernel, height),
-            small + own + sides,
-            [((2 * MARGIN + TILE, LANES), LOCAL), ((3, 2 * MARGIN, LANES), LOCAL)],
+            small + own + sides + [(lean, LOCAL)],
+            [((2 * MARGIN + TILE + lean_rows, LANES), LOCAL), ((3, 2 * MARGIN, LANES), LOCAL)],
             [room(n_edge, LANES)] * 3
             + [room(ITERS, n_edge, LANES)] * 3
             + [room(n_edge, LANES)] * 5,
         )
-        edge_near = moved(edge, "range", -1)
+        edge_near = moved(edge)
         received = []
         if more:
             (rest,) = call(
@@ -805,7 +813,7 @@
                 stages + [(done, LOCAL)],
                 [((height // 2, LANES), LOCAL)],
             )
-            received = [(moved(rest, "range", -1), LOCAL)]
+            received = [(moved(rest), LOCAL)]
         strip, wide = call(
             functools.partial(wide_kernel, height),
             small + own + ahead + sides,
@@ -817,7 +825,7 @@
             small[:1] + stages + [(x, LOCAL) for x in (done, wide, near)],
             [(field, LOCAL)] * 3,
         )
-        mixed = [(x, LOCAL) for x in (done, strip, lean_near, edge_near, *drafts)]
+        mixed = [(x, LOCAL) for x in (done, strip, edge_near, *drafts)]
         return tuple(
             call(
                 functools.partial(last_kernel, height, extra, more),

time: 31.8 us -> 27.1 us (0.85)
  the two profiles are of different devices: /device:TPU:29 before, /device:TPU:0 now
where the time goes in v1:
time: 27.1 us; the launch traced here: 26.9 us
  Pallas kernels  11.5 us (42%)
  waiting for transfers between devices  10.3 us (38%)
  starting transfers between devices  3.97 us (15%)
  between operations  0.83 us (3%)
  loops' own time  0.29 us (1%)
    pallas_call x6, Pallas kernels, call(): pl.pallas_call(kernel, in_specs=specs, out_specs=[space for _, space in o...  11.5 us
    ppermute x2, waiting for transfers between devices, moved(): lax.ppermute(x, 'range', [(i + 1, i) for i in range(lax.axis_size('range'...  10.3 us
    ppermute x2, starting transfers between devices, moved(): lax.ppermute(x, 'range', [(i + 1, i) for i in range(lax.axis_size('range'...  2.58 us
    ppermute x2, starting transfers between devices, swapped(): return lax.ppermute(x, 'depth', pairs + [(j, i) for i, j in pairs])  1.39 us
  transfers between devices with their start and end apart: 4, of which 2 were waited for; matrix products, arithmetic and copies ran while one was open for 0% of the time, Pallas kernels for 18%

profile of v1, /device:TPU:0, one launch (start us, length us, event | category | flops | bytes accessed | tf_op | source)
XLA Modules:
  0.0 26.9 jit_solution(13222644887091369517)
XLA Ops:
  0.6 4.4 %shard_map.127 = (f32[992,128]{1,0:T(8,128)}, f32[48,128]{1,0:T(8,128)S(1)}, f32[48,128]{1,0:T(8,128)S(1)}, f32[1024,128]{1,0:T(8,128)S(1)}, f32[1024,128]{1,0:T...) custom-call(s32[4]{0:T(128)} %refs_0_.1, ...), custom_call_target="tpu_custom_call" | custom-call | tf_op jit(solution)/shard_map/pallas_call | solution.py:735
  5.0 21.7 %conditional.1 = ((f32[1024,128]{1,0:T(8,128)}, f32[1024,128]{1,0:T(8,128)}, f32[1024,128]{1,0:T(8,128)})) conditional(s32[]{:T(128)} %bitcast.4, (f32[48,128]{1,0:T(8,128)S(1)}, f32[48,128]{1,0:T(8,128)S(1)}, f32[1024,128]{1,0:T(8,128)S(1)}, f32[1024,128]{1,0:T(8,128)S(1)}, f32[1024,128]{1,0:T(8,128)S(1)}, /*index=5*/f32[1024,128]{1,0:T(8,128)S(1)}, ...), branch_computations={%region_0.0_spmd, %region_1.0_spmd} | conditional | bytes 3735760 | solution.py:838
  5.0 1.3 %collective-permute-start.3 = (f32[992,128]{1,0:T(8,128)}, f32[992,128]{1,0:T(8,128)S(1)}, u32[]{:S(2)}, u32[]{:S(2)}) collective-permute-start(f32[992,128]{1,0:T(8,128)} %get-tuple-element.83), channel_id=1, source_target_pairs={{4,0},{8,4},{12,8},{16,12},{20,16},{24,20},{28,24},{5,1},{9,5},{13... | collective-permute-start | bytes 1523720 | tf_op jit(solution)/shard_map/cond/branch_0_fun/ppermute | solution.py:703
  6.3 0.7 %collective-permute-start = (f32[48,128]{1,0:T(8,128)S(1)}, f32[48,128]{1,0:T(8,128)S(1)}, u32[]{:S(2)}, u32[]{:S(2)}) collective-permute-start(f32[48,128]{1,0:T(8,128)S(1)} %get-tuple-element.72), channel_id=1, source_target_pairs={{0,1},{2,3},{1,0},{3,2},{4,5},{6,7},{5,4},{7,6},{8,9},{10,11},{9,8... | collective-permute-start | bytes 73736 | tf_op jit(solution)/shard_map/cond/branch_0_fun/ppermute | solution.py:708
  7.1 0.7 %collective-permute-start.1 = (f32[48,128]{1,0:T(8,128)S(1)}, f32[48,128]{1,0:T(8,128)S(1)}, u32[]{:S(2)}, u32[]{:S(2)}) collective-permute-start(f32[48,128]{1,0:T(8,128)S(1)} %get-tuple-element.73), channel_id=1, source_target_pairs={{1,2},{2,1},{5,6},{6,5},{9,10},{10,9},{13,14},{14,13},{17,18},{18,... | collective-permute-start | bytes 73736 | tf_op jit(solution)/shard_map/cond/branch_0_fun/ppermute | solution.py:708
  7.7 2.1 %branch_0_fun.5.refs_10_ = f32[184,128]{1,0:T(8,128)S(1)} custom-call(f32[1024,128]{1,0:T(8,128)S(1)} %get-tuple-element.67.refs_0_.refs_3_, f32[1024,128]{1,0:T(8,128)S(1)} %get-tuple-element.68.refs_1_.refs_4_, f32[1024,128]{1,0:T(8,128)S(1)} %get-tuple-element.69.refs_2_.refs_5_, f32[1024,128]{1,0:T(8,128)S(1)} %get-tuple-element.70.refs_3_.refs_6_, ...), custom_call_target="tpu_custom_call" | custom-call | tf_op jit(solution)/shard_map/cond/branch_0_fun/pallas_call | solution.py:735
  9.8 0.0 collective-permute-done.refs_8_.refs_10_
  9.8 0.0 collective-permute-done.1.refs_9_.refs_11_
  9.8 0.8 %branch_0_fun.6 = (f32[224,128]{1,0:T(8,128)S(1)}, f32[3,32,128]{2,1,0:T(8,128)S(1)}) custom-call(s32[4]{0:T(128)S(4)} %get-tuple-element.64.refs_0_, s32[2,8]{1,0:T(2,128)S(4)} %get-tuple-element.65.refs_1_, f32[4,8]{1,0:T(4,128)S(4)} %get-tuple-element.66.refs_2_, f32[1024,128]{1,0:T(8,128)S(1)} %get-tuple-element.67.refs_0_.refs_3_, ...), custom_call_target="tpu_custom_call" | custom-call | tf_op jit(solution)/shard_map/cond/branch_0_fun/pallas_call | solution.py:735
  10.6 1.3 %collective-permute-start.2 = (f32[224,128]{1,0:T(8,128)S(1)}, f32[224,128]{1,0:T(8,128)S(1)}, u32[]{:S(2)}, u32[]{:S(2)}) collective-permute-start(f32[224,128]{1,0:T(8,128)S(1)} %get-tuple-element.81), channel_id=1, source_target_pairs={{4,0},{8,4},{12,8},{16,12},{20,16},{24,20},{28,24},{5,1},{9,5},{13... | collective-permute-start | bytes 344072 | tf_op jit(solution)/shard_map/cond/branch_0_fun/ppermute | solution.py:703
  11.9 1.1 %branch_0_fun.7 = (f32[5,160,128]{2,1,0:T(8,128)S(1)}, f32[3,1056,128]{2,1,0:T(8,128)S(1)}) custom-call(s32[4]{0:T(128)S(4)} %get-tuple-element.64.refs_0_, s32[2,8]{1,0:T(2,128)S(4)} %get-tuple-element.65.refs_1_, f32[4,8]{1,0:T(4,128)S(4)} %get-tuple-element.66.refs_2_, f32[1024,128]{1,0:T(8,128)S(1)} %get-tuple-element.67.refs_0_.refs_3_, ...), custom_call_target="tpu_custom_call" | custom-call | tf_op jit(solution)/shard_map/cond/branch_0_fun/pallas_call | solution.py:735
  13.1 9.5 %collective-permute-done.3.refs_6_ = f32[992,128]{1,0:T(8,128)S(1)} collective-permute-done((f32[992,128]{1,0:T(8,128)}, f32[992,128]{1,0:T(8,128)S(1)}, u32[]{:S(2)}, u32[]{:S(2)}) %collective-permute-start.3) | collective-permute-done | bytes 507936 | tf_op jit(solution)/shard_map/cond/branch_0_fun/ppermute | solution.py:703
  22.5 0.7 %branch_0_fun.8 = (f32[1024,128]{1,0:T(8,128)S(1)}, f32[1024,128]{1,0:T(8,128)S(1)}, f32[1024,128]{1,0:T(8,128)S(1)}) custom-call(s32[4]{0:T(128)S(4)} %get-tuple-element.64.refs_0_, f32[4,1024,128]{2,1,0:T(8,128)S(1)} %get-tuple-element.74.refs_5_.refs_1_, f32[4,1024,128]{2,1,0:T(8,128)S(1)} %get-tuple-element.75.refs_6_.refs_2_, ...), custom_call_target="tpu_custom_call" | custom-call | tf_op jit(solution)/shard_map/cond/branch_0_fun/pallas_call | solution.py:735
  23.3 0.9 %collective-permute-done.2.refs_5_ = f32[224,128]{1,0:T(8,128)S(1)} collective-permute-done((f32[224,128]{1,0:T(8,128)S(1)}, f32[224,128]{1,0:T(8,128)S(1)}, u32[]{:S(2)}, u32[]{:S(2)}) %collective-permute-start.2) | collective-permute-done | bytes 114720 | tf_op jit(solution)/shard_map/cond/branch_0_fun/ppermute | solution.py:703
  24.2 2.3 %branch_0_fun.9 = (f32[1024,128]{1,0:T(8,128)}, f32[1024,128]{1,0:T(8,128)}, f32[1024,128]{1,0:T(8,128)}) custom-call(s32[4]{0:T(128)S(4)} %get-tuple-element.64.refs_0_, s32[2,8]{1,0:T(2,128)S(4)} %get-tuple-element.65.refs_1_, f32[4,8]{1,0:T(4,128)S(4)} %get-tuple-element.66.refs_2_, f32[3,32,128]{2,1,0:T(8,128)S(1)} %get-tuple-element.77.refs_4_.refs_3_, ...), custom_call_target="tpu_custom_call" | custom-call | tf_op jit(solution)/shard_map/cond/branch_0_fun/pallas_call | solution.py:735
Async XLA Ops:
  5.0 17.5 %collective-permute-start.3 = (f32[992,128]{1,0:T(8,128)}, f32[992,128]{1,0:T(8,128)S(1)}, u32[]{:S(2)}, u32[]{:S(2)}) collective-permute-start(f32[992,128]{1,0:T(8,128)} %get-tuple-element.83), channel_id=1, source_target_pairs={{4,0},{8,4},{12,8},{16,12},{20,16},{24,20},{28,24},{5,1},{9,5},{13... | collective-permute-start | bytes 1523720 | tf_op jit(solution)/shard_map/cond/branch_0_fun/ppermute | solution.py:703
  6.3 3.5 %collective-permute-start = (f32[48,128]{1,0:T(8,128)S(1)}, f32[48,128]{1,0:T(8,128)S(1)}, u32[]{:S(2)}, u32[]{:S(2)}) collective-permute-start(f32[48,128]{1,0:T(8,128)S(1)} %get-tuple-element.72), channel_id=1, source_target_pairs={{0,1},{2,3},{1,0},{3,2},{4,5},{6,7},{5,4},{7,6},{8,9},{10,11},{9,8... | collective-permute-start | bytes 73736 | tf_op jit(solution)/shard_map/cond/branch_0_fun/ppermute | solution.py:708
  7.1 2.8 %collective-permute-start.1 = (f32[48,128]{1,0:T(8,128)S(1)}, f32[48,128]{1,0:T(8,128)S(1)}, u32[]{:S(2)}, u32[]{:S(2)}) collective-permute-start(f32[48,128]{1,0:T(8,128)S(1)} %get-tuple-element.73), channel_id=1, source_target_pairs={{1,2},{2,1},{5,6},{6,5},{9,10},{10,9},{13,14},{14,13},{17,18},{18,... | collective-permute-start | bytes 73736 | tf_op jit(solution)/shard_map/cond/branch_0_fun/ppermute | solution.py:708
  10.6 13.5 %collective-permute-start.2 = (f32[224,128]{1,0:T(8,128)S(1)}, f32[224,128]{1,0:T(8,128)S(1)}, u32[]{:S(2)}, u32[]{:S(2)}) collective-permute-start(f32[224,128]{1,0:T(8,128)S(1)} %get-tuple-element.81), channel_id=1, source_target_pairs={{4,0},{8,4},{12,8},{16,12},{20,16},{24,20},{28,24},{5,1},{9,5},{13... | collective-permute-start | bytes 344072 | tf_op jit(solution)/shard_map/cond/branch_0_fun/ppermute | solution.py:703

commit v2 on v1

--- a/solution.py
+++ b/solution.py
@@ -14,6 +14,9 @@
 MARGIN = 16
 SKEW = 4
 WIDTH = 42
+NARROW = 32
+START = SKEW + WIDTH
+MORE = ((NARROW + SKEW, 0, 0), (START, 0, 0), (START + 10, 10, 4), (1 << 20, 18, 2))
 STRIP = 16
 BLOCKS = LANES // STRIP
 KEPT = LANES - STRIP // 2
@@ -78,30 +81,43 @@
 
 
 def find_sources(sources, first_row, places):
-    found = []
-    for k in range(sources.shape[1]):
+    def candidates(k):
+        found = []
         for row, lane, good in places(sources[0, k] - first_row, sources[1, k]):
-            good = jnp.logical_and(good, jnp.logical_and(lane >= 0, lane < LANES))
-            found.append((k, row, lane, good))
-    return found
+            good = jnp.logical_and(good, between(lane, 0, LANES))
+            found.append((row, lane, good))
+        return found
+
+    def look(k, seen):
+        for _, _, good in candidates(k):
+            seen = jnp.logical_or(seen, good)
+        return seen
+
+    return candidates, lax.fori_loop(0, sources.shape[1], look, jnp.bool_(False))
 
 
 def inject(field, found, wavelet, t, reach=None):
-    here_any = functools.reduce(jnp.logical_or, [good for _, _, _, good in found])
-
-    @pl.when(here_any)
+    candidates, seen = found
+
+    @pl.when(seen)
     def _():
         rows = lax.broadcasted_iota(jnp.int32, (TILE, LANES), 0)
         lanes = lane_ids(TILE)
-        for k, row, lane, good in found:
-            if reach is not None:
-                good = jnp.logical_and(good, lane % STRIP <= reach)
-
-            @pl.when(good)
-            def _(k=k, row=row, lane=lane):
-                at = pl.ds(pl.multiple_of((row // TILE) * TILE, TILE), TILE)
-                here = jnp.logical_and(rows == row % TILE, lanes == lane)
-                field[at, :] = field[at, :] + jnp.where(here, wavelet[t, k], 0.0)
+
+        def add(k, carry):
+            for row, lane, good in candidates(k):
+                if reach is not None:
+                    good = jnp.logical_and(good, lane % STRIP <= reach)
+
+                @pl.when(good)
+                def _(row=row, lane=lane):
+                    at = pl.ds(pl.multiple_of((row // TILE) * TILE, TILE), TILE)
+                    here = jnp.logical_and(rows == row % TILE, lanes == lane)
+                    field[at, :] = field[at, :] + jnp.where(here, wavelet[t, k], 0.0)
+
+            return carry
+
+        lax.fori_loop(0, wavelet.shape[1], add, 0)
 
 
 def left_steps(n, fields, coefs, stages, shifts, found, wavelet):
@@ -110,8 +126,8 @@
     offsets = offsets_of(shifts)
     at_start, _ = range_ends()
     for t in range(ITERS):
-        p, u, w = fields if t == 0 else (ps.at[t - 1], us.at[t - 1], ws.at[t - 1])
-        u_new, w_new, p_new = us.at[t], ws.at[t], ps.at[t]
+        p, u, w = fields if t == 0 else (ps[t - 1], us[t - 1], ws[t - 1])
+        u_new, w_new, p_new = us[t], ws[t], ps[t]
         wall = jnp.where(at_start, offsets[t], -1)
 
         def speeds(r, k):
@@ -142,31 +158,35 @@
             found = jnp.where(lanes <= t, parts[t], found)
         return found
 
-    a = pick([p0[here, :]] + [ps[t, here, :] for t in range(ITERS - 1)])
-    b = pick([us[t, here, :] for t in range(ITERS)])
-    c = pick([ws[t, here, :] for t in range(ITERS)])
+    a = pick([p0[here, :]] + [ps[t][here, :] for t in range(ITERS - 1)])
+    b = pick([us[t][here, :] for t in range(ITERS)])
+    c = pick([ws[t][here, :] for t in range(ITERS)])
     found = jnp.where(lanes < 3 * SKEW, roll(c, 2 * SKEW), roll(stiff, 3 * SKEW))
     found = jnp.where(lanes < 2 * SKEW, roll(b, SKEW), found)
     return jnp.where(lanes < SKEW, a, found)
 
 
-def packed(p, u, w):
+def packed(p, u, w, width=WIDTH):
     lanes = lane_ids(p.shape[0])
     found = jnp.where(
-        between(lanes, SKEW, SKEW + 2 * WIDTH), roll(u, WIDTH), roll(w, 2 * WIDTH)
+        between(lanes, SKEW, SKEW + 2 * width), roll(u, width), roll(w, 2 * width)
     )
-    return jnp.where(between(lanes, SKEW, SKEW + WIDTH), p, found)
+    return jnp.where(between(lanes, SKEW, SKEW + width), p, found)
 
 
 def finals(stages, here):
-    return [stage[ITERS - 1, here, :] for stage in stages]
+    return [stage[-1][here, :] for stage in stages]
+
+
+def staged(early, final):
+    return [[a.at[t] for t in range(ITERS - 1)] + [b] for a, b in zip(early, final)]
 
 
 def own_kernel(height, *refs):
     arrays, ahead = refs[3:8], refs[8:10]
-    plane, swap_one, swap_two = refs[10:13]
-    own, stages, scalars, flag = refs[13:18], refs[18:21], refs[21:24], refs[24]
-    ax, az, stiff, ends, sems, end_sems, scalar_sems = refs[25:]
+    swap_one, swap_two = refs[10:12]
+    own, stages, scalars = refs[12:17], staged(refs[17:20], refs[20:23]), refs[23:26]
+    flag, ax, az, stiff, ends, sems, end_sems, scalar_sems = refs[26:]
     shifts, sources, wavelet = scalars
     order = (4, 3, 0, 1, 2)
     copies = {k: pltpu.make_async_copy(arrays[k], own[k], sems.at[k]) for k in order}
@@ -197,16 +217,16 @@
     set_coefs(0, height - TILE, c, rho, ax, az, stiff)
     for copy in scalar_copies:
         copy.wait()
-    flag[0] = jnp.where(offsets_of(shifts)[ITERS] > SKEW + WIDTH, 1, 0)
+    total = offsets_of(shifts)[ITERS]
+    kind = jnp.int32(0)
+    for limit, _, _ in MORE[:-1]:
+        kind = kind + jnp.where(total > limit, 1, 0)
+    flag[0] = kind
     found = find_sources(sources, lax.axis_index("depth") * height, place)
     for k in (0, 1, 2):
         copies[k].wait()
     left_steps(height, (p, u, w), (ax, az, stiff), stages, shifts, found, wavelet)
 
-    def finish(r, k):
-        plane[pl.ds(r - MARGIN, k), :] = packed(*finals(stages, pl.ds(r, k)))
-
-    for_rows(MARGIN, height - MARGIN, finish)
     for copy in end_copies:
         copy.wait()
     even = lax.axis_index("depth") % 2 == 0
@@ -218,13 +238,30 @@
         swap_two[at, :] = jnp.where(even, top, low)
 
 
+def pack_kernel(height, low, *refs):
+    stages, plane = [[ref] for ref in refs[:3]], refs[3]
+    if not low:
+
+        def finish(r, k):
+            plane[pl.ds(r - MARGIN, k), :] = packed(*finals(stages, pl.ds(r, k)))
+
+        for_rows(MARGIN, height - MARGIN, finish)
+        return
+    each = (height - 2 * MARGIN) // 4
+    inner = between(lane_ids(each), SKEW, SKEW + 3 * NARROW)
+    spread = finals(stages, pl.ds(MARGIN + 3 * each, each))
+    for b in range(3):
+        part = packed(*finals(stages, pl.ds(MARGIN + b * each, each)), NARROW)
+        plane[pl.ds(b * each, each), :] = jnp.where(inner, part, roll(spread[b], 3 * NARROW))
+
+
 def own_stiff(own, here):
     speed = own[3][here, :]
     return TIME_STEP * (own[4][here, :] * speed * speed)
 
 
 def lean_kernel(height, *refs):
-    own, stages, lean = refs[:5], refs[5:8], refs[8]
+    own, stages, lean = refs[:5], staged(refs[5:8], refs[8:11]), refs[11]
     each = height // BLOCKS
     tiles = each // TILE + 2
 
@@ -287,7 +324,7 @@
     own, swap_one, swap_two, lean = refs[3:8], refs[8], refs[9], refs[10]
     out, done = refs[11:13]
     ax, az, stiff = refs[13:16]
-    stages, inner = refs[16:19], refs[19:24]
+    stages, inner = staged(refs[16:19], refs[19:22]), refs[22:27]
     seg = 3 * MARGIN
     n = 2 * seg
     low = height - 2 * MARGIN
@@ -473,36 +510,44 @@
             inject(p, found, wavelet, t)
 
 
-def rest_kernel(height, extra, *refs):
-    stages, done, out = refs[:3], refs[3], refs[4]
-    more = extra - SKEW - WIDTH
-    start = SKEW + WIDTH
-    half = height // 2
-
-    def read(row, k):
-        if isinstance(row, int) and row < MARGIN:
-            return [done[f, pl.ds(row, k), :] for f in range(3)]
-        if isinstance(row, int) and row >= height - MARGIN:
-            return [done[f, pl.ds(row - height + 2 * MARGIN, k), :] for f in range(3)]
-        return finals(stages, pl.ds(row, k))
+def rest_kernel(height, more, blocks, *refs):
+    stages, done, out = [[ref] for ref in refs[:3]], refs[3], refs[4]
+    each = height // blocks
+
+    def read(b, side, r, k):
+        if b == 0 and side < 0:
+            return [done[f, pl.ds(0, k), :] for f in range(3)]
+        if b == blocks - 1 and side > 0:
+            return [done[f, pl.ds(MARGIN, k), :] for f in range(3)]
+        return finals(stages, pl.ds(r + b * each, k))
 
     def join(fields):
         lanes = lane_ids(fields[0].shape[0])
-        found = jnp.where(lanes < start + 2 * more, roll(fields[1], more), roll(fields[2], 2 * more))
-        return jnp.where(lanes < start + more, fields[0], found)
-
-    def beside(r, k):
-        inner = between(lane_ids(k), start, start + 3 * more)
-        out[pl.ds(r, k), :] = jnp.where(inner, join(read(r, k)), roll(join(read(r + half, k)), LANES // 2))
-
-    beside(0, MARGIN)
-    for_rows(MARGIN, half - MARGIN, beside, 96)
-    beside(half - MARGIN, MARGIN)
-
-
-def mid_kernel(height, *refs):
+        found = jnp.where(lanes < START + 2 * more, roll(fields[1], more), roll(fields[2], 2 * more))
+        return jnp.where(lanes < START + more, fields[0], found)
+
+    for side, (low, high) in zip((-1, 0, 1), ((0, MARGIN), (MARGIN, each - MARGIN), (each - MARGIN, each))):
+
+        def beside(r, k, side=side):
+            lanes = lane_ids(k)
+            found = join(read(0, side, r, k))
+            for b in range(1, blocks):
+                part = roll(join(read(b, side, r, k)), LANES // blocks * b)
+                start = START + LANES // blocks * b
+                mine = between(lanes, start, start + 3 * more)
+                if start + 3 * more > LANES:
+                    mine = jnp.logical_or(lanes >= start, lanes < start + 3 * more - LANES)
+                    if start >= LANES:
+                        mine = between(lanes, start - LANES, start + 3 * more - LANES)
+                found = jnp.where(mine, part, found)
+            out[pl.ds(r, k), :] = found
+
+        for_rows(low, high, beside)
+
+
+def mid_kernel(height, low, *refs):
     shifts, stages, done, wide, near = refs[0], refs[1:4], refs[4], refs[5], refs[6]
-    built = refs[7:]
+    built = refs[-3:]
     _, at_end = range_ends()
     total = offsets_of(shifts)[ITERS]
     turn = LANES - total
@@ -511,14 +556,19 @@
     @pl.when(jnp.logical_not(at_end))
     def _():
         def build(r, k):
-            got = near[pl.ds(r - MARGIN, k), :]
             theirs = between(lane_ids(k), SKEW, total)
             for f in range(3):
-                mine = stages[f][ITERS - 1, pl.ds(r, k), :]
-                other = roll(got, -WIDTH * f) if f else got
+                mine = stages[f][pl.ds(r, k), :]
+                at, back = r - MARGIN, (NARROW if low else WIDTH) * f
+                if low and at >= 3 * each:
+                    at, back = f * each, 3 * NARROW
+                other = near[pl.ds(at, k), :]
+                other = roll(other, -back) if back else other
                 built[f][pl.ds(r, k), :] = pltpu.roll(jnp.where(theirs, other, mine), turn, 1)
 
-        for_rows(*inside, build)
+        each = (inside[1] - inside[0]) // 4
+        for start in range(*inside, each):
+            build(start, each)
 
     @pl.when(at_end)
     def _():
@@ -528,7 +578,7 @@
             for f in range(3):
                 part = roll(wide[f, pl.ds(r + MARGIN, k), :], LANES // 2)
                 if inside[0] <= r < inside[1]:
-                    mine = stages[f][ITERS - 1, pl.ds(r, k), :]
+                    mine = stages[f][pl.ds(r, k), :]
                 else:
                     mine = done[f, pl.ds(0 if r < MARGIN else MARGIN, k), :]
                 built[f][pl.ds(r, k), :] = pltpu.roll(jnp.where(inner, mine, part), turn, 1)
@@ -538,7 +588,8 @@
         build(height - MARGIN, MARGIN)
 
 
-def last_kernel(height, extra, far_too, *refs):
+def last_kernel(height, more, blocks, *refs):
+    far_too = more > 0
     shifts, sources, wavelet = refs[:3]
     done, strip, edge = refs[3:6]
     lean = edge.at[pl.ds(2 * MARGIN + TILE, edge.shape[0] - 2 * MARGIN - TILE)]
@@ -552,11 +603,9 @@
     each = height // BLOCKS
     tiles = each // TILE + 2
     n = (tiles + 2) * TILE
-    half = LANES // 2
     own_part = STRIP // 2
     total = offsets_of(shifts)[ITERS]
-    more = extra - SKEW - WIDTH
-    start = SKEW + WIDTH
+    start = START
     turn = LANES - total
 
     @pl.when(at_end)
@@ -571,8 +620,7 @@
     def _():
         lanes = lane_ids(TILE)
         inner = lanes % STRIP
-        mine, ghost = inner < own_part, inner < own_part + SKEW
-        fill = [0.0, 0.0, 0.0, 0.0, 1.0]
+        mine = inner < own_part
         six = edge[pl.ds(2 * MARGIN, TILE), :]
         for i in range(tiles):
             here = pl.ds((i + 1) * TILE, TILE)
@@ -597,8 +645,7 @@
             for ref, part in zip((gp, gu, gw), parts):
                 ref[here, :] = part
             for a, (ref, part) in enumerate(zip((p, u, w, stiff, rho), parts)):
-                other = jnp.where(ghost, part, fill[a])
-                ref[here, :] = jnp.where(mine, strip[a, here, :], other)
+                ref[here, :] = jnp.where(mine, strip[a, here, :], part)
         for e in (0, n - TILE):
             here = pl.ds(e, TILE)
             for ref in (p, u, w, stiff):
@@ -661,9 +708,9 @@
                 edges = [(high, MARGIN)]
 
             def far_values(row, k):
-                if row < height // 2:
-                    return rest[pl.ds(row, k), :]
-                return roll(rest[pl.ds(row - height // 2, k), :], half)
+                b = row // (height // blocks)
+                found = rest[pl.ds(row - b * (height // blocks), k), :]
+                return roll(found, -LANES // blocks * b) if b else found
 
             for row, side in edges:
                 here, there = pl.ds(row, MARGIN), pl.ds(side, MARGIN)
@@ -761,6 +808,7 @@
     height, breadth = pressure.shape
     extra = ahead_speed.shape[1]
     assert breadth == LANES and 2 * extra == LANES and height % 512 == 0
+    assert START + MORE[-1][1] == extra
     arrays = [(x, REMOTE) for x in (pressure, vel_range, vel_depth, sound_speed, density)]
     ahead = [(x.T, REMOTE) for x in (ahead_speed, ahead_density)]
     small = [(shifts, REMOTE), (sources.T, REMOTE), (wavelet.T, REMOTE)]
@@ -773,10 +821,10 @@
     found = call(
         functools.partial(own_kernel, height),
         small + arrays + ahead,
-        [((height - 2 * MARGIN, LANES), LOCAL)]
-        + [((6 * TILE, LANES), LOCAL)] * 2
+        [((6 * TILE, LANES), LOCAL)] * 2
         + [(field, LOCAL)] * 5
-        + [((ITERS, *field), LOCAL)] * 3
+        + [((ITERS - 1, *field), LOCAL)] * 3
+        + [(field, LOCAL)] * 3
         + scalars
         + [(((1,), jnp.int32), SCALAR)],
         [room(*field)] * 3 + [room(2, LANES, LANES), dma((5,)), dma((2, 2)), dma((3,))],
@@ -787,12 +835,19 @@
     n_wide = height + 2 * MARGIN
     n_strip = (tiles + 2) * TILE
 
-    def finish(more, ahead, plane, swap_one, swap_two, *found):
+    def finish(kind, ahead, swap_one, swap_two, *found):
+        _, more, blocks = MORE[kind]
         ahead = [(x, REMOTE) for x in ahead]
         own = [(x, LOCAL) for x in found[:5]]
-        stages = [(x, LOCAL) for x in found[5:8]]
-        small = [(x, SCALAR) for x in found[8:]]
-        near = moved(plane)
+        stages = [(x, LOCAL) for x in found[5:11]]
+        last = stages[3:]
+        small = [(x, SCALAR) for x in found[11:]]
+        (plane,) = call(
+            functools.partial(pack_kernel, height, kind == 0),
+            last,
+            [(((4 if kind else 3) * (height - 2 * MARGIN) // 4, LANES), LOCAL)],
+        )
+        near = [(moved(plane), LOCAL)]
         sides = [(swapped(swap_one, 0), LOCAL), (swapped(swap_two, 1), LOCAL)]
         (lean,) = call(
             functools.partial(lean_kernel, height), own + stages, [((lean_rows, LANES), LOCAL)]
@@ -802,16 +857,16 @@
             small + own + sides + [(lean, LOCAL)],
             [((2 * MARGIN + TILE + lean_rows, LANES), LOCAL), ((3, 2 * MARGIN, LANES), LOCAL)],
             [room(n_edge, LANES)] * 3
-            + [room(ITERS, n_edge, LANES)] * 3
-            + [room(n_edge, LANES)] * 5,
+            + [room(ITERS - 1, n_edge, LANES)] * 3
+            + [room(n_edge, LANES)] * 8,
         )
         edge_near = moved(edge)
         received = []
         if more:
             (rest,) = call(
-                functools.partial(rest_kernel, height, extra),
-                stages + [(done, LOCAL)],
-                [((height // 2, LANES), LOCAL)],
+                functools.partial(rest_kernel, height, more, blocks),
+                last + [(done, LOCAL)],
+                [((height // blocks, LANES), LOCAL)],
             )
             received = [(moved(rest), LOCAL)]
         strip, wide = call(
@@ -821,24 +876,23 @@
             [room(n_wide, LANES)] * 5 + [room(2, extra, height), dma((2,))],
         )
         drafts = call(
-            functools.partial(mid_kernel, height),
-            small[:1] + stages + [(x, LOCAL) for x in (done, wide, near)],
+            functools.partial(mid_kernel, height, kind == 0),
+            small[:1] + last + [(done, LOCAL), (wide, LOCAL)] + near,
             [(field, LOCAL)] * 3,
         )
         mixed = [(x, LOCAL) for x in (done, strip, edge_near, *drafts)]
         return tuple(
             call(
-                functools.partial(last_kernel, height, extra, more),
+                functools.partial(last_kernel, height, more, blocks),
                 small + mixed + received,
                 [(field, REMOTE)] * 3,
                 [room(*field)] * 3 + [room(n_strip, LANES)] * 10 + [dma((3, BLOCKS))],
             )
         )
 
-    return lax.cond(
-        found[-1].reshape(()) > 0,
-        functools.partial(finish, True),
-        functools.partial(finish, False),
+    return lax.switch(
+        found[-1].reshape(()),
+        [functools.partial(finish, kind) for kind in range(len(MORE))],
         [x for x, _ in ahead],
         *found[:-1],
     )

time: 27.1 us -> 27.5 us (1.015)
  waiting for transfers between devices: 10.3 us -> 9.02 us
  Pallas kernels: 11.5 us -> 12.3 us
  loops' own time: 0.29 us -> 0.69 us
  starting transfers between devices: 3.97 us -> 4.37 us
    ppermute x2, waiting for transfers between devices: 10.3 us -> 9.02 us  [moved(): lax.ppermute(x, 'range', [(i + 1, i) for i in range(lax.axis_size('range'...]
    pallas_call x6 -> x7, Pallas kernels: 11.5 us -> 12.3 us  [call(): pl.pallas_call(kernel, in_specs=specs, out_specs=[space for _, space in o...]
    another operation x1, loops' own time: 0.29 us -> 0.69 us  [shards(): lax.switch(found[-1].reshape(()), [functools.partial(finish, kind) for ki...]
    ppermute x2, starting transfers between devices: 1.39 us -> 1.79 us  [swapped(): return lax.ppermute(x, 'depth', pairs + [(j, i) for i, j in pairs])]
  transfers between devices with their start and end apart: 4 -> 4, of which waited for: 2 -> 2; matrix products, arithmetic and copies ran while one was open for 0% -> 0% of each run, Pallas kernels for 18% -> 20%
where the time goes in v2:
time: 27.5 us; the launch traced here: 27.3 us
  Pallas kernels  12.3 us (45%)
  waiting for transfers between devices  9.02 us (33%)
  starting transfers between devices  4.37 us (16%)
  between operations  0.89 us (3%)
  loops' own time  0.69 us (3%)
    pallas_call x7, Pallas kernels, call(): pl.pallas_call(kernel, in_specs=specs, out_specs=[space for _, space in o...  12.3 us
    ppermute x2, waiting for transfers between devices, moved(): lax.ppermute(x, 'range', [(i + 1, i) for i in range(lax.axis_size('range'...  9.02 us
    ppermute x2, starting transfers between devices, moved(): lax.ppermute(x, 'range', [(i + 1, i) for i in range(lax.axis_size('range'...  2.58 us
    ppermute x2, starting transfers between devices, swapped(): return lax.ppermute(x, 'depth', pairs + [(j, i) for i, j in pairs])  1.79 us
    another operation x1, loops' own time, shards(): lax.switch(found[-1].reshape(()), [functools.partial(finish, kind) for ki...  0.69 us
  transfers between devices with their start and end apart: 4, of which 2 were waited for; matrix products, arithmetic and copies ran while one was open for 0% of the time, Pallas kernels for 20%

profile of v2, /device:TPU:0, one launch (start us, length us, event | category | flops | bytes accessed | tf_op | source)
XLA Modules:
  0.0 27.3 jit_solution(3075184222932034062)
XLA Ops:
  0.6 3.9 %shard_map.133 = (f32[48,128]{1,0:T(8,128)S(1)}, f32[48,128]{1,0:T(8,128)S(1)}, f32[1024,128]{1,0:T(8,128)S(1)}, f32[1024,128]{1,0:T(8,128)S(1)}, f32[1024,128]{...) custom-call(s32[4]{0:T(128)} %refs_0_.1, ...), custom_call_target="tpu_custom_call" | custom-call | tf_op jit(solution)/shard_map/pallas_call | solution.py:782
  4.5 22.5 %conditional.1 = ((f32[1024,128]{1,0:T(8,128)}, f32[1024,128]{1,0:T(8,128)}, f32[1024,128]{1,0:T(8,128)})) conditional(s32[]{:T(128)} %bitcast.4, (f32[48,128]{1,0:T(8,128)S(1)}, f32[48,128]{1,0:T(8,128)S(1)}, f32[1024,128]{1,0:T(8,128)S(1)}, f32[1024,128]{1,0:T(8,128)S(1)}, f32[1024,128]{1,0:T(8,128)S(1)}, ...), branch_computations={%region_0.0_spmd, %region_1.0_spmd, %region_2.0_spmd, %region_3.0_... | conditional | bytes 3735760 | solution.py:893
  4.6 0.3 %branch_1_fun.9 = f32[992,128]{1,0:T(8,128)S(1)} custom-call(f32[1024,128]{1,0:T(8,128)S(1)} %get-tuple-element.182.refs_8_.refs_0_.refs_1_, f32[1024,128]{1,0:T(8,128)S(1)} %get-tuple-element.183.refs_9_.refs_1_.refs_2_, f32[1024,128]{1,0:T(8,128)S(1)} %get-tuple-element.184.refs_10_.refs_2_.refs_3_), custom_call_target="tpu_custom_call" | custom-call | tf_op jit(solution)/shard_map/cond/branch_1_fun/pallas_call | solution.py:782
  4.9 1.3 %collective-permute-start.7 = (f32[992,128]{1,0:T(8,128)S(1)}, f32[992,128]{1,0:T(8,128)S(1)}, u32[]{:S(2)}, u32[]{:S(2)}) collective-permute-start(f32[992,128]{1,0:T(8,128)S(1)} %branch_1_fun.9), channel_id=1, source_target_pairs={{4,0},{8,4},{12,8},{16,12},{20,16},{24,20},{28,24},{5,1},{9,5},{13... | collective-permute-start | bytes 1523720 | tf_op jit(solution)/shard_map/cond/branch_1_fun/ppermute | solution.py:750
  6.2 1.1 %collective-permute-start.4 = (f32[48,128]{1,0:T(8,128)S(1)}, f32[48,128]{1,0:T(8,128)S(1)}, u32[]{:S(2)}, u32[]{:S(2)}) collective-permute-start(f32[48,128]{1,0:T(8,128)S(1)} %get-tuple-element.177), channel_id=1, source_target_pairs={{0,1},{2,3},{1,0},{3,2},{4,5},{6,7},{5,4},{7,6},{8,9},{10,11},{9,8... | collective-permute-start | bytes 73736 | tf_op jit(solution)/shard_map/cond/branch_1_fun/ppermute | solution.py:755
  7.3 0.7 %collective-permute-start.5 = (f32[48,128]{1,0:T(8,128)S(1)}, f32[48,128]{1,0:T(8,128)S(1)}, u32[]{:S(2)}, u32[]{:S(2)}) collective-permute-start(f32[48,128]{1,0:T(8,128)S(1)} %get-tuple-element.178), channel_id=1, source_target_pairs={{1,2},{2,1},{5,6},{6,5},{9,10},{10,9},{13,14},{14,13},{17,18},{18,... | collective-permute-start | bytes 73736 | tf_op jit(solution)/shard_map/cond/branch_1_fun/ppermute | solution.py:755
  8.0 2.1 %branch_1_fun.6.refs_10_ = f32[184,128]{1,0:T(8,128)S(1)} custom-call(f32[1024,128]{1,0:T(8,128)S(1)} %get-tuple-element.172.refs_0_.refs_3_, f32[1024,128]{1,0:T(8,128)S(1)} %get-tuple-element.173.refs_1_.refs_4_, f32[1024,128]{1,0:T(8,128)S(1)} %get-tuple-element.174.refs_2_.refs_5_, f32[1024,128]{1,0:T(8,128)S(1)} %get-tuple-element.175.refs_3_.refs_6_, ...), custom_call_target="tpu_custom_call" | custom-call | tf_op jit(solution)/shard_map/cond/branch_1_fun/pallas_call | solution.py:782
  10.1 0.0 collective-permute-done.4.refs_8_.refs_10_
  10.1 0.0 collective-permute-done.5.refs_9_.refs_11_
  10.1 1.0 %branch_1_fun.7 = (f32[224,128]{1,0:T(8,128)S(1)}, f32[3,32,128]{2,1,0:T(8,128)S(1)}) custom-call(s32[4]{0:T(128)S(4)} %get-tuple-element.169.refs_0_, s32[2,8]{1,0:T(2,128)S(4)} %get-tuple-element.170.refs_1_, f32[4,8]{1,0:T(4,128)S(4)} %get-tuple-element.171.refs_2_, f32[1024,128]{1,0:T(8,128)S(1)} %get-tuple-element.172.refs_0_.refs_3_, ...), custom_call_target="tpu_custom_call" | custom-call | tf_op jit(solution)/shard_map/cond/branch_1_fun/pallas_call | solution.py:782
  11.1 1.3 %collective-permute-start.6 = (f32[224,128]{1,0:T(8,128)S(1)}, f32[224,128]{1,0:T(8,128)S(1)}, u32[]{:S(2)}, u32[]{:S(2)}) collective-permute-start(f32[224,128]{1,0:T(8,128)S(1)} %get-tuple-element.189), channel_id=1, source_target_pairs={{4,0},{8,4},{12,8},{16,12},{20,16},{24,20},{28,24},{5,1},{9,5},{13... | collective-permute-start | bytes 344072 | tf_op jit(solution)/shard_map/cond/branch_1_fun/ppermute | solution.py:750
  12.4 1.4 %branch_1_fun.8 = (f32[5,160,128]{2,1,0:T(8,128)S(1)}, f32[3,1056,128]{2,1,0:T(8,128)S(1)}) custom-call(s32[4]{0:T(128)S(4)} %get-tuple-element.169.refs_0_, s32[2,8]{1,0:T(2,128)S(4)} %get-tuple-element.170.refs_1_, f32[4,8]{1,0:T(4,128)S(4)} %get-tuple-element.171.refs_2_, f32[1024,128]{1,0:T(8,128)S(1)} %get-tuple-element.172.refs_0_.refs_3_, ...), custom_call_target="tpu_custom_call" | custom-call | tf_op jit(solution)/shard_map/cond/branch_1_fun/pallas_call | solution.py:782
  13.8 8.4 %collective-permute-done.7.refs_6_ = f32[992,128]{1,0:T(8,128)S(1)} collective-permute-done((f32[992,128]{1,0:T(8,128)S(1)}, f32[992,128]{1,0:T(8,128)S(1)}, u32[]{:S(2)}, u32[]{:S(2)}) %collective-permute-start.7) | collective-permute-done | bytes 507936 | tf_op jit(solution)/shard_map/cond/branch_1_fun/ppermute | solution.py:750
  22.2 1.0 %branch_1_fun.10 = (f32[1024,128]{1,0:T(8,128)S(1)}, f32[1024,128]{1,0:T(8,128)S(1)}, f32[1024,128]{1,0:T(8,128)S(1)}) custom-call(s32[4]{0:T(128)S(4)} %get-tuple-element.169.refs_0_, f32[1024,128]{1,0:T(8,128)S(1)} %get-tuple-element.182.refs_8_.refs_0_.refs_1_, f32[1024,128]{1,0:T(8,128)S(1)} %get-tuple-element.183.refs_9_.refs_1_.refs_2_, ...), custom_call_target="tpu_custom_call" | custom-call | tf_op jit(solution)/shard_map/cond/branch_1_fun/pallas_call | solution.py:782
  23.2 0.6 %collective-permute-done.6.refs_5_ = f32[224,128]{1,0:T(8,128)S(1)} collective-permute-done((f32[224,128]{1,0:T(8,128)S(1)}, f32[224,128]{1,0:T(8,128)S(1)}, u32[]{:S(2)}, u32[]{:S(2)}) %collective-permute-start.6) | collective-permute-done | bytes 114720 | tf_op jit(solution)/shard_map/cond/branch_1_fun/ppermute | solution.py:750
  23.8 2.6 %branch_1_fun.11 = (f32[1024,128]{1,0:T(8,128)}, f32[1024,128]{1,0:T(8,128)}, f32[1024,128]{1,0:T(8,128)}) custom-call(s32[4]{0:T(128)S(4)} %get-tuple-element.169.refs_0_, s32[2,8]{1,0:T(2,128)S(4)} %get-tuple-element.170.refs_1_, f32[4,8]{1,0:T(4,128)S(4)} %get-tuple-element.171.refs_2_, f32[3,32,128]{2,1,0:T(8,128)S(1)} %get-tuple-element.185.refs_4_.refs_3_, ...), custom_call_target="tpu_custom_call" | custom-call | tf_op jit(solution)/shard_map/cond/branch_1_fun/pallas_call | solution.py:782
Async XLA Ops:
  4.9 17.3 %collective-permute-start.7 = (f32[992,128]{1,0:T(8,128)S(1)}, f32[992,128]{1,0:T(8,128)S(1)}, u32[]{:S(2)}, u32[]{:S(2)}) collective-permute-start(f32[992,128]{1,0:T(8,128)S(1)} %branch_1_fun.9), channel_id=1, source_target_pairs={{4,0},{8,4},{12,8},{16,12},{20,16},{24,20},{28,24},{5,1},{9,5},{13... | collective-permute-start | bytes 1523720 | tf_op jit(solution)/shard_map/cond/branch_1_fun/ppermute | solution.py:750
  6.2 3.9 %collective-permute-start.4 = (f32[48,128]{1,0:T(8,128)S(1)}, f32[48,128]{1,0:T(8,128)S(1)}, u32[]{:S(2)}, u32[]{:S(2)}) collective-permute-start(f32[48,128]{1,0:T(8,128)S(1)} %get-tuple-element.177), channel_id=1, source_target_pairs={{0,1},{2,3},{1,0},{3,2},{4,5},{6,7},{5,4},{7,6},{8,9},{10,11},{9,8... | collective-permute-start | bytes 73736 | tf_op jit(solution)/shard_map/cond/branch_1_fun/ppermute | solution.py:755
  7.3 2.8 %collective-permute-start.5 = (f32[48,128]{1,0:T(8,128)S(1)}, f32[48,128]{1,0:T(8,128)S(1)}, u32[]{:S(2)}, u32[]{:S(2)}) collective-permute-start(f32[48,128]{1,0:T(8,128)S(1)} %get-tuple-element.178), channel_id=1, source_target_pairs={{1,2},{2,1},{5,6},{6,5},{9,10},{10,9},{13,14},{14,13},{17,18},{18,... | collective-permute-start | bytes 73736 | tf_op jit(solution)/shard_map/cond/branch_1_fun/ppermute | solution.py:755
  11.1 12.7 %collective-permute-start.6 = (f32[224,128]{1,0:T(8,128)S(1)}, f32[224,128]{1,0:T(8,128)S(1)}, u32[]{:S(2)}, u32[]{:S(2)}) collective-permute-start(f32[224,128]{1,0:T(8,128)S(1)} %get-tuple-element.189), channel_id=1, source_target_pairs={{4,0},{8,4},{12,8},{16,12},{20,16},{24,20},{28,24},{5,1},{9,5},{13... | collective-permute-start | bytes 344072 | tf_op jit(solution)/shard_map/cond/branch_1_fun/ppermute | solution.py:750

commit v3 on v2

--- a/solution.py
+++ b/solution.py
@@ -80,10 +80,10 @@
     for_rows(start, stop, coefs)
 
 
-def find_sources(sources, first_row, places):
+def find_sources(sources, height, places, seen=None):
     def candidates(k):
         found = []
-        for row, lane, good in places(sources[0, k] - first_row, sources[1, k]):
+        for row, lane, good in places(height, sources[0, k] - lax.axis_index("depth") * height, sources[1, k]):
             good = jnp.logical_and(good, between(lane, 0, LANES))
             found.append((row, lane, good))
         return found
@@ -93,7 +93,42 @@
             seen = jnp.logical_or(seen, good)
         return seen
 
-    return candidates, lax.fori_loop(0, sources.shape[1], look, jnp.bool_(False))
+    if seen is None:
+        seen = lax.fori_loop(0, sources.shape[1], look, jnp.bool_(False))
+    return candidates, seen
+
+
+def own_place(height, row, col):
+    return [(row, col - lax.axis_index("range") * LANES, between(row, 0, height))]
+
+
+def edge_place(height, row, col):
+    low, seg = height - 2 * MARGIN, 3 * MARGIN
+    upper = between(row, -TILE, 2 * MARGIN)
+    lower = between(row, low, height + TILE)
+    local = jnp.where(upper, row + MARGIN, row - low + seg)
+    lane = col - lax.axis_index("range") * LANES
+    return [(local, lane, jnp.logical_or(upper, lower))]
+
+
+def wide_place(height, row, col):
+    good = between(row, -TILE, height + TILE)
+    return [(row + MARGIN, col - lax.axis_index("range") * LANES - LANES // 2, good)]
+
+
+def strip_place(height, row, col):
+    each = height // BLOCKS
+    col = col - lax.axis_index("range") * LANES - KEPT
+    inside = between(col, 0, STRIP)
+    inside = jnp.logical_and(inside, between(row, -TILE, height + TILE))
+    b = (row + TILE) // each
+    local = row + TILE - b * each
+    one = jnp.logical_and(inside, b < BLOCKS)
+    two = jnp.logical_and(inside, jnp.logical_and(b > 0, local < 2 * TILE))
+    return [
+        (local + TILE, STRIP * b + col, one),
+        (local + each + TILE, STRIP * (b - 1) + col, two),
+    ]
 
 
 def inject(field, found, wavelet, t, reach=None):
@@ -186,17 +221,17 @@
     arrays, ahead = refs[3:8], refs[8:10]
     swap_one, swap_two = refs[10:12]
     own, stages, scalars = refs[12:17], staged(refs[17:20], refs[20:23]), refs[23:26]
-    flag, ax, az, stiff, ends, sems, end_sems, scalar_sems = refs[26:]
+    seen, flag, ax, az, stiff, ends, sems, end_sems, scalar_sems = refs[26:]
     shifts, sources, wavelet = scalars
     order = (4, 3, 0, 1, 2)
     copies = {k: pltpu.make_async_copy(arrays[k], own[k], sems.at[k]) for k in order}
-    for k in order:
-        copies[k].start()
     scalar_copies = [
         pltpu.make_async_copy(refs[k], scalars[k], scalar_sems.at[k]) for k in range(3)
     ]
     for copy in scalar_copies:
         copy.start()
+    for k in order:
+        copies[k].start()
     end_copies = []
     for side, start in enumerate((0, height - LANES)):
         for f in range(2):
@@ -209,12 +244,6 @@
             end_copies.append(copy)
     p, u, w, c, rho = own
 
-    def place(row, col):
-        return [(row, col - lax.axis_index("range") * LANES, between(row, 0, height))]
-
-    copies[4].wait()
-    copies[3].wait()
-    set_coefs(0, height - TILE, c, rho, ax, az, stiff)
     for copy in scalar_copies:
         copy.wait()
     total = offsets_of(shifts)[ITERS]
@@ -222,7 +251,12 @@
     for limit, _, _ in MORE[:-1]:
         kind = kind + jnp.where(total > limit, 1, 0)
     flag[0] = kind
-    found = find_sources(sources, lax.axis_index("depth") * height, place)
+    for j, places in enumerate((edge_place, wide_place, strip_place)):
+        seen[j] = jnp.where(find_sources(sources, height, places)[1], 1, 0)
+    found = find_sources(sources, height, own_place)
+    copies[4].wait()
+    copies[3].wait()
+    set_coefs(0, height - TILE, c, rho, ax, az, stiff)
     for k in (0, 1, 2):
         copies[k].wait()
     left_steps(height, (p, u, w), (ax, az, stiff), stages, shifts, found, wavelet)
@@ -320,7 +354,8 @@
 
 
 def edge_kernel(height, *refs):
-    shifts, sources, wavelet = refs[:3]
+    shifts, sources, wavelet, seen = refs[:4]
+    refs = refs[1:]
     own, swap_one, swap_two, lean = refs[3:8], refs[8], refs[9], refs[10]
     out, done = refs[11:13]
     ax, az, stiff = refs[13:16]
@@ -344,14 +379,7 @@
     at = pl.ds(TILE, TILE)
     az[at, :] = jnp.where(at_top, 0.0, az[at, :])
 
-    def place(row, col):
-        upper = between(row, -TILE, 2 * MARGIN)
-        lower = between(row, low, height + TILE)
-        local = jnp.where(upper, row + MARGIN, row - low + seg)
-        lane = col - lax.axis_index("range") * LANES
-        return [(local, lane, jnp.logical_or(upper, lower))]
-
-    found = find_sources(sources, lax.axis_index("depth") * height, place)
+    found = find_sources(sources, height, edge_place, seen[0] > 0)
     left_steps(n, (p, u, w), (ax, az, stiff), stages, shifts, found, wavelet)
     for side, start in enumerate((MARGIN, seg + MARGIN)):
         fields = finals(stages, pl.ds(start, MARGIN))
@@ -385,7 +413,8 @@
 
 
 def wide_kernel(height, *refs):
-    shifts, sources, wavelet = refs[:3]
+    shifts, sources, wavelet, seen = refs[:4]
+    refs = refs[1:]
     own, ahead, swap_one, swap_two = refs[3:8], refs[8:10], refs[10], refs[11]
     strip, out = refs[12:14]
     p, u, w = out.at[0], out.at[1], out.at[2]
@@ -479,11 +508,7 @@
         at = pl.ds(TILE, TILE)
         az[at, :] = jnp.where(at_top, 0.0, az[at, :])
 
-        def place(row, col):
-            good = between(row, -TILE, height + TILE)
-            return [(row + MARGIN, col - lax.axis_index("range") * LANES - half, good)]
-
-        found = find_sources(sources, lax.axis_index("depth") * height, place)
+        found = find_sources(sources, height, wide_place, seen[1] > 0)
         offsets = offsets_of(shifts)
         for t in range(ITERS):
             edge = half - 1 + offsets[t]
@@ -590,7 +615,8 @@
 
 def last_kernel(height, more, blocks, *refs):
     far_too = more > 0
-    shifts, sources, wavelet = refs[:3]
+    shifts, sources, wavelet, seen = refs[:4]
+    refs = refs[1:]
     done, strip, edge = refs[3:6]
     lean = edge.at[pl.ds(2 * MARGIN + TILE, edge.shape[0] - 2 * MARGIN - TILE)]
     drafts = refs[6:9]
@@ -655,20 +681,7 @@
         at = pl.ds(TILE, TILE)
         az[at, :] = jnp.where(jnp.logical_and(at_top, lane_ids(TILE) < STRIP), 0.0, az[at, :])
 
-        def place(row, col):
-            col = col - lax.axis_index("range") * LANES - KEPT
-            inside = between(col, 0, STRIP)
-            inside = jnp.logical_and(inside, between(row, -TILE, height + TILE))
-            b = (row + TILE) // each
-            local = row + TILE - b * each
-            one = jnp.logical_and(inside, b < BLOCKS)
-            two = jnp.logical_and(inside, jnp.logical_and(b > 0, local < 2 * TILE))
-            return [
-                (local + TILE, STRIP * b + col, one),
-                (local + each + TILE, STRIP * (b - 1) + col, two),
-            ]
-
-        found = find_sources(sources, lax.axis_index("depth") * height, place)
+        found = find_sources(sources, height, strip_place, seen[2] > 0)
         for t in range(ITERS):
             taken = own_part + t
 
@@ -826,7 +839,7 @@
         + [((ITERS - 1, *field), LOCAL)] * 3
         + [(field, LOCAL)] * 3
         + scalars
-        + [(((1,), jnp.int32), SCALAR)],
+        + [(((3,), jnp.int32), SCALAR), (((1,), jnp.int32), SCALAR)],
         [room(*field)] * 3 + [room(2, LANES, LANES), dma((5,)), dma((2, 2)), dma((3,))],
     )
     tiles = height // BLOCKS // TILE + 2

time: 27.5 us -> 27.1 us (0.985)
  Pallas kernels: 12.3 us -> 11.8 us
    pallas_call x7, Pallas kernels: 12.3 us -> 11.8 us  [call(): pl.pallas_call(kernel, in_specs=specs, out_specs=[space for _, space in o...]
where the time goes in v3:
time: 27.1 us; the launch traced here: 26.9 us
  Pallas kernels  11.8 us (44%)
  waiting for transfers between devices  9.26 us (34%)
  starting transfers between devices  4.37 us (16%)
  between operations  0.87 us (3%)
  loops' own time  0.61 us (2%)
    pallas_call x7, Pallas kernels, call(): pl.pallas_call(kernel, in_specs=specs, out_specs=[space for _, space in o...  11.8 us
    ppermute x2, waiting for transfers between devices, moved(): lax.ppermute(x, 'range', [(i + 1, i) for i in range(lax.axis_size('range'...  9.25 us
    ppermute x2, starting transfers between devices, moved(): lax.ppermute(x, 'range', [(i + 1, i) for i in range(lax.axis_size('range'...  2.58 us
    ppermute x2, starting transfers between devices, swapped(): return lax.ppermute(x, 'depth', pairs + [(j, i) for i, j in pairs])  1.79 us
    another operation x1, loops' own time, shards(): lax.switch(found[-1].reshape(()), [functools.partial(finish, kind) for ki...  0.61 us
  transfers between devices with their start and end apart: 4, of which 2 were waited for; matrix products, arithmetic and copies ran while one was open for 0% of the time, Pallas kernels for 20%

profile of v3, /device:TPU:0, one launch (start us, length us, event | category | flops | bytes accessed | tf_op | source)
XLA Modules:
  0.0 26.9 jit_solution(11112843914225445550)
XLA Ops:
  0.6 3.9 %shard_map.133 = (f32[48,128]{1,0:T(8,128)S(1)}, f32[48,128]{1,0:T(8,128)S(1)}, f32[1024,128]{1,0:T(8,128)S(1)}, f32[1024,128]{1,0:T(8,128)S(1)}, f32[1024,128]{...) custom-call(s32[4]{0:T(128)} %refs_0_.1, ...), custom_call_target="tpu_custom_call" | custom-call | tf_op jit(solution)/shard_map/pallas_call | solution.py:795
  4.6 22.1 %conditional.1 = ((f32[1024,128]{1,0:T(8,128)}, f32[1024,128]{1,0:T(8,128)}, f32[1024,128]{1,0:T(8,128)})) conditional(s32[]{:T(128)} %bitcast.4, (f32[48,128]{1,0:T(8,128)S(1)}, f32[48,128]{1,0:T(8,128)S(1)}, f32[1024,128]{1,0:T(8,128)S(1)}, f32[1024,128]{1,0:T(8,128)S(1)}, f32[1024,128]{1,0:T(8,128)S(1)}, ...), branch_computations={%region_0.0_spmd, %region_1.0_spmd, %region_2.0_spmd, %region_3.0_... | conditional | bytes 3735760 | solution.py:906
  4.6 0.3 %branch_1_fun.9 = f32[992,128]{1,0:T(8,128)S(1)} custom-call(f32[1024,128]{1,0:T(8,128)S(1)} %get-tuple-element.192.refs_8_.refs_0_.refs_1_, f32[1024,128]{1,0:T(8,128)S(1)} %get-tuple-element.193.refs_9_.refs_1_.refs_2_, f32[1024,128]{1,0:T(8,128)S(1)} %get-tuple-element.194.refs_10_.refs_2_.refs_3_), custom_call_target="tpu_custom_call" | custom-call | tf_op jit(solution)/shard_map/cond/branch_1_fun/pallas_call | solution.py:795
  4.9 1.3 %collective-permute-start.7 = (f32[992,128]{1,0:T(8,128)S(1)}, f32[992,128]{1,0:T(8,128)S(1)}, u32[]{:S(2)}, u32[]{:S(2)}) collective-permute-start(f32[992,128]{1,0:T(8,128)S(1)} %branch_1_fun.9), channel_id=1, source_target_pairs={{4,0},{8,4},{12,8},{16,12},{20,16},{24,20},{28,24},{5,1},{9,5},{13... | collective-permute-start | bytes 1523720 | tf_op jit(solution)/shard_map/cond/branch_1_fun/ppermute | solution.py:763
  6.2 1.1 %collective-permute-start.4 = (f32[48,128]{1,0:T(8,128)S(1)}, f32[48,128]{1,0:T(8,128)S(1)}, u32[]{:S(2)}, u32[]{:S(2)}) collective-permute-start(f32[48,128]{1,0:T(8,128)S(1)} %get-tuple-element.187), channel_id=1, source_target_pairs={{0,1},{2,3},{1,0},{3,2},{4,5},{6,7},{5,4},{7,6},{8,9},{10,11},{9,8... | collective-permute-start | bytes 73736 | tf_op jit(solution)/shard_map/cond/branch_1_fun/ppermute | solution.py:768
  7.4 0.7 %collective-permute-start.5 = (f32[48,128]{1,0:T(8,128)S(1)}, f32[48,128]{1,0:T(8,128)S(1)}, u32[]{:S(2)}, u32[]{:S(2)}) collective-permute-start(f32[48,128]{1,0:T(8,128)S(1)} %get-tuple-element.188), channel_id=1, source_target_pairs={{1,2},{2,1},{5,6},{6,5},{9,10},{10,9},{13,14},{14,13},{17,18},{18,... | collective-permute-start | bytes 73736 | tf_op jit(solution)/shard_map/cond/branch_1_fun/ppermute | solution.py:768
  8.0 2.1 %branch_1_fun.6.refs_11_ = f32[184,128]{1,0:T(8,128)S(1)} custom-call(f32[1024,128]{1,0:T(8,128)S(1)} %get-tuple-element.182.refs_0_.refs_4_, f32[1024,128]{1,0:T(8,128)S(1)} %get-tuple-element.183.refs_1_.refs_5_, f32[1024,128]{1,0:T(8,128)S(1)} %get-tuple-element.184.refs_2_.refs_6_, f32[1024,128]{1,0:T(8,128)S(1)} %get-tuple-element.185.refs_3_.refs_7_, ...), custom_call_target="tpu_custom_call" | custom-call | tf_op jit(solution)/shard_map/cond/branch_1_fun/pallas_call | solution.py:795
  10.2 0.0 collective-permute-done.4.refs_9_.refs_11_
  10.2 0.0 collective-permute-done.5.refs_10_.refs_12_
  10.2 0.8 %branch_1_fun.7 = (f32[224,128]{1,0:T(8,128)S(1)}, f32[3,32,128]{2,1,0:T(8,128)S(1)}) custom-call(s32[4]{0:T(128)S(4)} %get-tuple-element.178.refs_0_, s32[2,8]{1,0:T(2,128)S(4)} %get-tuple-element.179.refs_1_, f32[4,8]{1,0:T(4,128)S(4)} %get-tuple-element.180.refs_2_, s32[3]{0:T(128)S(4)} %get-tuple-element.181.refs_3_, ...), custom_call_target="tpu_custom_call" | custom-call | tf_op jit(solution)/shard_map/cond/branch_1_fun/pallas_call | solution.py:795
  11.0 1.3 %collective-permute-start.6 = (f32[224,128]{1,0:T(8,128)S(1)}, f32[224,128]{1,0:T(8,128)S(1)}, u32[]{:S(2)}, u32[]{:S(2)}) collective-permute-start(f32[224,128]{1,0:T(8,128)S(1)} %get-tuple-element.199), channel_id=1, source_target_pairs={{4,0},{8,4},{12,8},{16,12},{20,16},{24,20},{28,24},{5,1},{9,5},{13... | collective-permute-start | bytes 344072 | tf_op jit(solution)/shard_map/cond/branch_1_fun/ppermute | solution.py:763
  12.3 1.3 %branch_1_fun.8 = (f32[5,160,128]{2,1,0:T(8,128)S(1)}, f32[3,1056,128]{2,1,0:T(8,128)S(1)}) custom-call(s32[4]{0:T(128)S(4)} %get-tuple-element.178.refs_0_, s32[2,8]{1,0:T(2,128)S(4)} %get-tuple-element.179.refs_1_, f32[4,8]{1,0:T(4,128)S(4)} %get-tuple-element.180.refs_2_, s32[3]{0:T(128)S(4)} %get-tuple-element.181.refs_3_, ...), custom_call_target="tpu_custom_call" | custom-call | tf_op jit(solution)/shard_map/cond/branch_1_fun/pallas_call | solution.py:795
  13.6 8.6 %collective-permute-done.7.refs_6_ = f32[992,128]{1,0:T(8,128)S(1)} collective-permute-done((f32[992,128]{1,0:T(8,128)S(1)}, f32[992,128]{1,0:T(8,128)S(1)}, u32[]{:S(2)}, u32[]{:S(2)}) %collective-permute-start.7) | collective-permute-done | bytes 507936 | tf_op jit(solution)/shard_map/cond/branch_1_fun/ppermute | solution.py:763
  22.3 1.0 %branch_1_fun.10 = (f32[1024,128]{1,0:T(8,128)S(1)}, f32[1024,128]{1,0:T(8,128)S(1)}, f32[1024,128]{1,0:T(8,128)S(1)}) custom-call(s32[4]{0:T(128)S(4)} %get-tuple-element.178.refs_0_, f32[1024,128]{1,0:T(8,128)S(1)} %get-tuple-element.192.refs_8_.refs_0_.refs_1_, f32[1024,128]{1,0:T(8,128)S(1)} %get-tuple-element.193.refs_9_.refs_1_.refs_2_, ...), custom_call_target="tpu_custom_call" | custom-call | tf_op jit(solution)/shard_map/cond/branch_1_fun/pallas_call | solution.py:795
  23.3 0.6 %collective-permute-done.6.refs_6_ = f32[224,128]{1,0:T(8,128)S(1)} collective-permute-done((f32[224,128]{1,0:T(8,128)S(1)}, f32[224,128]{1,0:T(8,128)S(1)}, u32[]{:S(2)}, u32[]{:S(2)}) %collective-permute-start.6) | collective-permute-done | bytes 114720 | tf_op jit(solution)/shard_map/cond/branch_1_fun/ppermute | solution.py:763
  23.9 2.3 %branch_1_fun.11 = (f32[1024,128]{1,0:T(8,128)}, f32[1024,128]{1,0:T(8,128)}, f32[1024,128]{1,0:T(8,128)}) custom-call(s32[4]{0:T(128)S(4)} %get-tuple-element.178.refs_0_, s32[2,8]{1,0:T(2,128)S(4)} %get-tuple-element.179.refs_1_, f32[4,8]{1,0:T(4,128)S(4)} %get-tuple-element.180.refs_2_, s32[3]{0:T(128)S(4)} %get-tuple-element.181.refs_3_, ...), custom_call_target="tpu_custom_call" | custom-call | tf_op jit(solution)/shard_map/cond/branch_1_fun/pallas_call | solution.py:795
Async XLA Ops:
  4.9 17.3 %collective-permute-start.7 = (f32[992,128]{1,0:T(8,128)S(1)}, f32[992,128]{1,0:T(8,128)S(1)}, u32[]{:S(2)}, u32[]{:S(2)}) collective-permute-start(f32[992,128]{1,0:T(8,128)S(1)} %branch_1_fun.9), channel_id=1, source_target_pairs={{4,0},{8,4},{12,8},{16,12},{20,16},{24,20},{28,24},{5,1},{9,5},{13... | collective-permute-start | bytes 1523720 | tf_op jit(solution)/shard_map/cond/branch_1_fun/ppermute | solution.py:763
  6.2 3.9 %collective-permute-start.4 = (f32[48,128]{1,0:T(8,128)S(1)}, f32[48,128]{1,0:T(8,128)S(1)}, u32[]{:S(2)}, u32[]{:S(2)}) collective-permute-start(f32[48,128]{1,0:T(8,128)S(1)} %get-tuple-element.187), channel_id=1, source_target_pairs={{0,1},{2,3},{1,0},{3,2},{4,5},{6,7},{5,4},{7,6},{8,9},{10,11},{9,8... | collective-permute-start | bytes 73736 | tf_op jit(solution)/shard_map/cond/branch_1_fun/ppermute | solution.py:768
  7.4 2.8 %collective-permute-start.5 = (f32[48,128]{1,0:T(8,128)S(1)}, f32[48,128]{1,0:T(8,128)S(1)}, u32[]{:S(2)}, u32[]{:S(2)}) collective-permute-start(f32[48,128]{1,0:T(8,128)S(1)} %get-tuple-element.188), channel_id=1, source_target_pairs={{1,2},{2,1},{5,6},{6,5},{9,10},{10,9},{13,14},{14,13},{17,18},{18,... | collective-permute-start | bytes 73736 | tf_op jit(solution)/shard_map/cond/branch_1_fun/ppermute | solution.py:768
  11.0 12.9 %collective-permute-start.6 = (f32[224,128]{1,0:T(8,128)S(1)}, f32[224,128]{1,0:T(8,128)S(1)}, u32[]{:S(2)}, u32[]{:S(2)}) collective-permute-start(f32[224,128]{1,0:T(8,128)S(1)} %get-tuple-element.199), channel_id=1, source_target_pairs={{4,0},{8,4},{12,8},{16,12},{20,16},{24,20},{28,24},{5,1},{9,5},{13... | collective-permute-start | bytes 344072 | tf_op jit(solution)/shard_map/cond/branch_1_fun/ppermute | solution.py:763
